TPU v7x, 32 devices: a whole 2x2x4 slice. The times are simulated.
32 devices in a mesh: gx: 8 (over y, x, core), gy: 4 (over z).
Axes of the slice: x: 2, y: 2, z: 4, core: 2. Of those that a mesh axis runs over, the one named last changes fastest.
Arguments:
- volts: float32 [32, 4, 64, 512], P(None, None, 'gx', 'gy'), may hold values from -6 to 6
- cap: float32 [4, 64, 512], P(None, 'gx', 'gy'), may hold values from 0.05 to 1
- cond_x: float32 [4, 64, 512], P(None, 'gx', 'gy'), may hold values from 0.5 to 2
- cond_y: float32 [4, 64, 512], P(None, 'gx', 'gy'), may hold values from 0.5 to 2
- via: float32 [4, 64, 512], P(None, 'gx', 'gy'), may hold values from 0.2 to 2
- waveforms: float32 [64, 64], replicated, may hold values from -6 to 6
- placement: int32 [262144, 1], P(('gx', 'gy')), may hold values from 0 to 31; in each aligned block of 8192 rows (0 to 8191, 8192 to 16383, ...) at most 512 rows name the same one
- cells: int32 [262144], P(('gx', 'gy')), may hold values from 0 to 1023
- wave_ids: int32 [262144], P(('gx', 'gy')), may hold values from 0 to 63
- amps: float32 [262144], P(('gx', 'gy')), may hold values from 0.5 to 4
Outputs:
- volts_out: float32 [32, 4, 64, 512], P(None, None, 'gx', 'gy')
- residual: float32 [32, 4, 64, 512], P(None, None, 'gx', 'gy')
Inputs may be any that keep to these rules, and one draw needn't show every extreme that they name: `placement`: in each device's block of 8192 rows no tile is named more than 512 times, a bound that some block reaches.
All inputs are finite; a program needn't handle non-finite values.
Results may differ from a plain program's by a relative error of at most 0.0029.
Values may be sent and summed in bfloat16 or wider, within the bound.
A program may use at most 64 MiB of HBM per device.

v0:
```python
import functools

import jax
import jax.numpy as jnp
from jax import lax
from jax.experimental import pallas as pl
from jax.experimental.pallas import tpu as pltpu
from jax.sharding import PartitionSpec as P

ITERS = 3
LANES = 128
MESH = pl.DeviceIdType.MESH
HIGHEST = lax.Precision.HIGHEST
NT = (((1,), (1,)), ((), ()))
TN = (((0,), (0,)), ((), ()))
F32 = jnp.float32
BF16 = jnp.bfloat16


def split3(x):
    first = x.astype(BF16).astype(F32)
    rest = x - first
    second = rest.astype(BF16).astype(F32)
    return first, second, rest - second


def rows_iota(rows, cols):
    return lax.broadcasted_iota(jnp.int32, (rows, cols), 0)


def bin_kernel(devices, capacity, target_ref, cell_ref, wave_ref, amp_ref, out_ref, acc_ref):
    blocks, width = target_ref.shape
    rows = out_ref.shape[1]
    before = (
        rows_iota(width, width) < lax.broadcasted_iota(jnp.int32, (width, width), 1)
    ).astype(F32).astype(BF16)
    acc_ref[...] = jnp.zeros_like(acc_ref)

    def step(b, base):
        target = target_ref[pl.ds(b, 1), :]
        hits = (rows_iota(devices, width) == target).astype(F32)
        ahead = jnp.dot(hits.astype(BF16), before, preferred_element_type=F32)
        position = jnp.sum(hits * (ahead + base), axis=0, keepdims=True)
        slot = target * capacity + position.astype(jnp.int32)
        row_hits = rows_iota(rows, width) == (slot >> 7)
        lane_hits = (rows_iota(LANES, width) == (slot & 127)).astype(F32).astype(BF16)
        code = cell_ref[pl.ds(b, 1), :] * 64 + wave_ref[pl.ds(b, 1), :]
        parts = split3(amp_ref[pl.ds(b, 1), :]) + (
            (code >> 8).astype(F32),
            (code & 255).astype(F32),
        )
        for i, part in enumerate(parts):
            left = jnp.where(row_hits, part, 0.0).astype(BF16)
            acc_ref[i] += lax.dot_general(left, lane_hits, NT, preferred_element_type=F32)
        return base + jnp.sum(hits, axis=1, keepdims=True)

    lax.fori_loop(0, blocks, step, jnp.zeros((devices, 1), F32), unroll=2)
    out_ref[0] = (acc_ref[2] + acc_ref[1]) + acc_ref[0]
    out_ref[1] = acc_ref[3] * 256.0 + acc_ref[4]


def bin_instances(devices, capacity, target, cells, wave_ids, amps):
    width = 512
    shape = (target.shape[0] // width, width)
    rows = devices * capacity // LANES
    return pl.pallas_call(
        functools.partial(bin_kernel, devices, capacity),
        out_shape=jax.ShapeDtypeStruct((2, rows, LANES), F32),
        in_specs=[pl.BlockSpec(memory_space=pltpu.VMEM)] * 4,
        out_specs=pl.BlockSpec(memory_space=pltpu.VMEM),
        scratch_shapes=[pltpu.VMEM((5, rows, LANES), F32)],
        name="bin",
    )(*[x.reshape(shape) for x in (target, cells, wave_ids, amps)])


def inject_kernel(parts, arrived_ref, wave_ref, out_ref, acc_ref):
    sources, width = arrived_ref.shape[1:]
    kinds = wave_ref.shape[1]
    outs = wave_ref.shape[0]
    low_count = out_ref.shape[1] // parts
    table = jnp.concatenate(split3(wave_ref[...]), axis=0).astype(BF16)
    acc_ref[...] = jnp.zeros_like(acc_ref)

    def step(i, carry):
        amp = arrived_ref[0, pl.ds(i, 1), :]
        code = arrived_ref[1, pl.ds(i, 1), :].astype(jnp.int32)
        cell = code >> 6
        low, high = cell % low_count, cell // low_count
        kind_hits = (rows_iota(kinds, width) == (code & 63)).astype(F32).astype(BF16)
        picked = jnp.dot(table, kind_hits, preferred_element_type=F32)
        wave = (picked[2 * outs :] + picked[outs : 2 * outs]) + picked[:outs]
        currents = (wave * amp).astype(BF16).astype(F32)
        low_hits = (rows_iota(low_count, width) == low).astype(F32).astype(BF16)
        left = jnp.concatenate(
            [jnp.where(high == h, currents, 0.0).astype(BF16) for h in range(parts)], axis=0
        )
        acc_ref[...] += lax.dot_general(left, low_hits, NT, preferred_element_type=F32)
        return carry

    lax.fori_loop(0, sources, step, 0, unroll=2)
    for h in range(parts):
        out_ref[:, h * low_count : (h + 1) * low_count] = acc_ref[h * outs : (h + 1) * outs]


def inject(arrived, waveforms, die_cells):
    parts = 4
    return pl.pallas_call(
        functools.partial(inject_kernel, parts),
        out_shape=jax.ShapeDtypeStruct((waveforms.shape[0], die_cells), F32),
        in_specs=[pl.BlockSpec(memory_space=pltpu.VMEM)] * 2,
        out_specs=pl.BlockSpec(memory_space=pltpu.VMEM),
        scratch_shapes=[pltpu.VMEM((parts * waveforms.shape[0], die_cells // parts), F32)],
        name="inject",
    )(arrived, waveforms)


def eliminate(mats):
    size = mats[0].shape[0]
    rows = rows_iota(size, mats[0].shape[1])
    for k in range(size):
        fresh = []
        for m in mats:
            row = m[k : k + 1, :] / m[k : k + 1, k : k + 1]
            fresh.append(jnp.where(rows == k, row, m - m[:, k : k + 1] * row))
        mats = fresh
    return mats


def beside(left, right):
    size = left.shape[0]
    return jnp.concatenate([left, right, jnp.zeros((size, LANES - 2 * size), F32)], axis=1)


def small(a, b, dims=(((1,), (0,)), ((), ()))):
    return lax.dot_general(a, b, dims, precision=HIGHEST, preferred_element_type=F32)


def grid_kernel(
    nx, ny, steps, layers, tile_x,
    v_in, inj, coef, v, r,
    d, image, xs, xl, ys, yl, gs, gl, hs, hl,
    xsend, xrecv, ysend, yrecv, gsend, grecv, hsend, hrecv,
):
    gx, gy = lax.axis_index("gx"), lax.axis_index("gy")
    size = v.shape[0]
    count = layers * tile_x
    lane = lax.broadcasted_iota(jnp.int32, (size, LANES), 1)

    barrier = pltpu.get_barrier_semaphore()
    for axis, me, n in (("gx", gx, nx), ("gy", gy, ny)):
        for j in range(1, n):
            pl.semaphore_signal(
                barrier, inc=1, device_id={axis: lax.rem(me + j, n)}, device_id_type=MESH
            )
    pl.semaphore_wait(barrier, nx + ny - 2)

    def block(ref, c):
        return ref[:, c * LANES : (c + 1) * LANES]

    def exchange(src, e):
        for l in range(layers):
            at = slice(l * LANES, (l + 1) * LANES)
            xs[e, 0, :, at] = block(src, l * tile_x + tile_x - 1)
            xs[e, 1, :, at] = block(src, l * tile_x)
        copies = []
        for side, step in ((0, 1), (1, nx - 1)):
            copies.append(pltpu.make_async_remote_copy(
                xs.at[e, side], xl.at[e, side], xsend.at[e, side], xrecv.at[e, side],
                device_id={"gx": lax.rem(gx + step, nx)}, device_id_type=MESH,
            ))
            copies[-1].start()
        last = jnp.zeros((size, LANES), F32)
        first = last
        for c in range(count):
            f = block(src, c)
            last = jnp.where(lane == c, pltpu.roll(f, (c + 1) % LANES, 1), last)
            first = jnp.where(lane == c, pltpu.roll(f, c, 1) if c else f, first)
        ys[e, 0] = last
        ys[e, 1] = first
        for side, step in ((0, 1), (1, ny - 1)):
            copies.append(pltpu.make_async_remote_copy(
                ys.at[e, side], yl.at[e, side], ysend.at[e, side], yrecv.at[e, side],
                device_id={"gy": lax.rem(gy + step, ny)}, device_id_type=MESH,
            ))
            copies[-1].start()
        for copy in copies:
            copy.wait()

    def stencil(src, e, own, dst, finish):
        y_low, y_high = yl[e, 0], yl[e, 1]
        for c in range(count):
            l, x = divmod(c, tile_x)
            f = block(src, c)
            at = slice(l * LANES, (l + 1) * LANES)

            def k(i):
                return coef[i, c : c + 1, :]

            high = block(src, c + 1) if x + 1 < tile_x else xl[e, 1, :, at]
            low = block(src, c - 1) if x else xl[e, 0, :, at]
            total = k(own) * f - k(2) * high - k(3) * low
            after = jnp.where(
                lane == LANES - 1, pltpu.roll(y_high, LANES - 1 - c, 1), pltpu.roll(f, LANES - 1, 1)
            )
            ahead = jnp.where(
                lane == 0, pltpu.roll(y_low, LANES - c, 1) if c else y_low, pltpu.roll(f, 1, 1)
            )
            total = total - k(4) * after - k(5) * ahead
            if l + 1 < layers:
                total = total - k(6) * block(src, c + tile_x)
            if l:
                total = total - k(7) * block(src, c - tile_x)
            dst[:, c * LANES : (c + 1) * LANES] = finish(c, total)

    def start_all(send, land, e, ssem, rsem, axis, me, n):
        copies = []
        for j in range(1, n):
            copies.append(pltpu.make_async_remote_copy(
                send.at[e], land.at[e, j], ssem.at[e, j], rsem.at[e, j],
                device_id={axis: lax.rem(me + j, n)}, device_id_type=MESH,
            ))
            copies[-1].start()
        return copies

    def finish_all(copies, own, land, e, n):
        for copy in copies:
            copy.wait()
        total = own
        for j in range(1, n):
            total = total + land[e, j]
        return total

    def update(dst, base, coefs, field, sign):
        for c in range(layers):
            at = slice(c * tile_x * LANES, (c + 1) * tile_x * LANES)
            term = small(coefs, field[:, at], TN)
            dst[:, at] = base[:, at] + term if sign > 0 else base[:, at] - term

    v[...] = v_in[...]
    eye = (rows_iota(size, size) == lax.broadcasted_iota(jnp.int32, (size, size), 1)).astype(F32)
    pad = jnp.zeros((size, LANES - 3 * size), F32)

    def time_step(step, carry):
        e = step * (ITERS + 1)
        exchange(v, e)

        def residual_of(c, total):
            if c < tile_x:
                total = total + inj[pl.ds(pl.multiple_of(step * size, size), size),
                                    c * LANES : (c + 1) * LANES]
            return -total

        stencil(v, e, 1, r, residual_of)
        norm = None
        for sweep in range(ITERS):
            direction = d if sweep else r
            e = step * (ITERS + 1) + sweep + 1
            g = step * ITERS + sweep
            exchange(direction, e)
            stencil(direction, e, 0, image, lambda c, total: total)
            curve = small(direction[...], image[...], NT)
            if sweep + 1 < ITERS:
                square = small(image[...], image[...], NT)
                other = small(r[...], image[...] if sweep else r[...], NT)
                own = jnp.concatenate([curve, other, square, pad], axis=1)
            else:
                own = jnp.concatenate([curve, jnp.zeros((size, LANES - size), F32)], axis=1)
            gs[g] = own
            copies = start_all(gs, gl, g, gsend, grecv, "gx", gx, nx)
            inverse = None
            if sweep and sweep + 1 < ITERS:
                (inverse,) = eliminate([beside(norm, eye)])
            own = finish_all(copies, own, gl, g, nx)
            hs[g] = own
            copies = start_all(hs, hl, g, hsend, hrecv, "gy", gy, ny)
            total = finish_all(copies, own, hl, g, ny)
            curve = total[:, :size]
            cross = total[:, size : 2 * size]
            square = total[:, 2 * size : 3 * size]
            if sweep == 0:
                norm, cross = cross, curve
                solved, inverse = eliminate([beside(curve, norm), beside(norm, eye)])
            else:
                (solved,) = eliminate([beside(curve, norm)])
            step_coef = solved[:, size : 2 * size]
            update(v, v, step_coef, direction, 1)
            update(r, r, step_coef, image, -1) if sweep else None
            if sweep + 1 < ITERS:
                cross_term = small(cross, step_coef)
                cross_flip = small(step_coef, cross, (((0,), (1,)), ((), ())))
                square_term = small(step_coef, small(square, step_coef), TN)
                new = norm - cross_term - cross_flip + square_term
                turn = small(inverse[:, size : 2 * size], new)
                if sweep:
                    update(d, r, turn, d, 1)
                else:
                    update(d, r, turn, r, 1)
                    update(d, d, step_coef, image, -1)
                    update(r, r, step_coef, image, -1)
                norm = new
        return carry

    lax.fori_loop(0, steps, time_step, 0)


def solve_grid(nx, ny, steps, layers, tile_x, volts, injected, coef):
    size, width = volts.shape
    halos, grams = steps * (ITERS + 1), steps * ITERS
    dma = pltpu.SemaphoreType.DMA
    return pl.pallas_call(
        functools.partial(grid_kernel, nx, ny, steps, layers, tile_x),
        out_shape=[jax.ShapeDtypeStruct(volts.shape, F32)] * 2,
        in_specs=[pl.BlockSpec(memory_space=pltpu.VMEM)] * 3,
        out_specs=[pl.BlockSpec(memory_space=pltpu.VMEM)] * 2,
        scratch_shapes=[
            pltpu.VMEM(volts.shape, F32),
            pltpu.VMEM(volts.shape, F32),
            pltpu.VMEM((halos, 2, size, layers * LANES), F32),
            pltpu.VMEM((halos, 2, size, layers * LANES), F32),
            pltpu.VMEM((halos, 2, size, LANES), F32),
            pltpu.VMEM((halos, 2, size, LANES), F32),
            pltpu.VMEM((grams, size, LANES), F32),
            pltpu.VMEM((grams, nx, size, LANES), F32),
            pltpu.VMEM((grams, size, LANES), F32),
            pltpu.VMEM((grams, ny, size, LANES), F32),
            dma((halos, 2)), dma((halos, 2)), dma((halos, 2)), dma((halos, 2)),
            dma((grams, nx)), dma((grams, nx)), dma((grams, ny)), dma((grams, ny)),
        ],
        compiler_params=pltpu.CompilerParams(
            collective_id=0, has_side_effects=True, vmem_limit_bytes=48 * 1024 * 1024
        ),
        name="grid",
    )(volts, injected, coef)


def shifted(x, axis):
    length = lax.axis_size(axis)
    return lax.ppermute(x, axis, [(i, i + 1) for i in range(length - 1)])


def body(volts, cap, cond_x, cond_y, via, waveforms, placement, cells, wave_ids, amps):
    nx, ny = lax.axis_size("gx"), lax.axis_size("gy")
    devices = nx * ny
    scenarios, layers, tile_x, tile_y = volts.shape
    steps = waveforms.shape[0] // scenarios
    capacity = 2 * cells.shape[0] // devices
    slots = bin_instances(devices, capacity, placement[:, 0], cells, wave_ids, amps)
    arrived = lax.all_to_all(
        slots.reshape(2, devices, capacity), ("gx", "gy"), split_axis=1, concat_axis=1, tiled=True
    )
    injected = inject(arrived, waveforms, tile_x * tile_y)
    rim_x = shifted(cond_x[:, -1:, :], "gx")
    rim_y = shifted(cond_y[:, :, -1:], "gy")
    x_low = jnp.concatenate([rim_x, cond_x[:, :-1, :]], axis=1)
    y_low = jnp.concatenate([rim_y, cond_y[:, :, :-1]], axis=2)
    via_low = jnp.concatenate([jnp.zeros_like(via[:1]), via[:-1]], axis=0)
    at_x = lax.broadcasted_iota(jnp.int32, cond_x.shape, 1) + lax.axis_index("gx") * tile_x
    at_y = lax.broadcasted_iota(jnp.int32, cond_y.shape, 2) + lax.axis_index("gy") * tile_y
    x_next = jnp.where(at_x == nx * tile_x - 1, 0.0, cond_x)
    y_next = jnp.where(at_y == ny * tile_y - 1, 0.0, cond_y)
    around = cond_x + x_low + cond_y + y_low + via + via_low
    coef = jnp.stack([cap + around, around, x_next, x_low, y_next, y_low, via, via_low])
    coef = coef.reshape(8, layers * tile_x, tile_y)
    out, residual = solve_grid(
        nx, ny, steps, layers, tile_x, volts.reshape(scenarios, -1), injected, coef
    )
    return out.reshape(volts.shape), residual.reshape(volts.shape)


def solution(mesh):
    grid = P(None, "gx", "gy")
    field = P(None, None, "gx", "gy")
    flat = P(("gx", "gy"))
    return jax.shard_map(
        body,
        mesh=mesh,
        in_specs=(field, grid, grid, grid, grid, P(), P(("gx", "gy"), None), flat, flat, flat),
        out_specs=(field, field),
        check_vma=False,
    )
```

profile of v0, /device:TPU:0, one launch (start us, length us, event | category | flops | bytes accessed | tf_op | source)
XLA Modules:
  0.0 176.1 jit_solution(17816120511334309407)
XLA Ops:
  0.6 0.0 copy-start.5
  0.6 0.7 slice.15
  1.4 2.4 %collective-permute-start = (f32[4,1,128]{2,1,0:T(1,128)S(1)}, f32[4,1,128]{2,1,0:T(1,128)S(1)}, u32[]{:S(2)}, u32[]{:S(2)}) collective-permute-start(f32[4,1,128]{2,1,0:T(1,128)S(1)} %slice.15), channel_id=1, source_target_pairs={{0,4},{4,8},{8,12},{12,16},{16,20},{20,24},{24,28},{1,5},{5,9},{9,... | collective-permute-start | bytes 6152 | tf_op jit(solution)/shard_map/ppermute | solution.py:338
  3.8 0.8 slice.17
  4.6 4.3 %collective-permute-start.1 = (f32[4,8,1]{2,1,0:T(8,128)S(1)}, f32[4,8,1]{2,1,0:T(8,128)S(1)}, u32[]{:S(2)}, u32[]{:S(2)}) collective-permute-start(f32[4,8,1]{2,1,0:T(8,128)S(1)} %slice.17), channel_id=1, source_target_pairs={{0,1},{1,2},{2,3},{4,5},{5,6},{6,7},{8,9},{9,10},{10,11},{12,13},{... | collective-permute-start | bytes 392 | tf_op jit(solution)/shard_map/ppermute | solution.py:338
  8.8 0.5 broadcast.13
  9.4 0.0 copy-done.5
  9.4 0.7 reduce.3
  10.1 0.0 copy-start.6
  10.1 0.6 reshape_squeeze.3.target_ref
  10.7 0.1 copy-done.6
  10.9 0.0 copy-start.7
  10.9 0.6 reshape.43.cell_ref
  11.5 0.1 copy-done.7
  11.6 0.0 copy-start.8
  11.6 0.6 reshape.44.wave_ref
  12.2 0.2 copy-done.8
  12.4 0.6 reshape.45.amp_ref
  13.0 0.0 copy-start.1
  13.0 9.8 %bin.1 = f32[2,128,128]{2,1,0:T(8,128)} custom-call(s32[16,512]{1,0:T(8,128)} %reshape_squeeze.3.target_ref, s32[16,512]{1,0:T(8,128)} %reshape.43.cell_ref, s32[16,512]{1,0:T(8,128)} %reshape.44.wave_ref, f32[16,512]{1,0:T(8,128)} %reshape.45.amp_ref), custom_call_target="tpu_custom_call" | custom-call | tf_op jit(solution)/shard_map/bin/pallas_call | solution.py:66
  22.8 0.9 reshape.46
  23.7 0.8 copy.12
  24.5 5.0 %all-to-all-start = ((f32[2,32,512]{2,0,1:T(2,128)}), f32[2,32,512]{2,0,1:T(2,128)S(1)}, u32[]{:S(2)}, u32[]{:S(2)}) async-start(f32[2,32,512]{2,0,1:T(2,128)} %copy.12), calls=%async_computation | async-start | bytes 262144 | tf_op jit(solution)/shard_map/all_to_all | solution.py:348
  29.5 0.0 copy-start.4
  29.5 0.7 copy-done.4
  30.2 0.0 copy-done.1
  30.2 0.0 copy-start.2
  30.2 0.0 copy-start.3
  30.2 0.0 copy-start.9
  30.2 0.3 copy.18
  30.5 0.0 collective-permute-done.1
  30.6 0.0 collective-permute-done
  30.6 0.4 copy-done.2
  30.9 0.0 copy-done.3
  30.9 0.0 copy-done.9
  31.0 0.1 constant_dynamic-update-slice_fusion.7
  31.0 0.1 constant_dynamic-update-slice_fusion.5
  31.1 0.1 constant_dynamic-update-slice_fusion.2
  31.2 6.6 %all-to-all-done = f32[2,32,512]{2,0,1:T(2,128)S(1)} async-done(((f32[2,32,512]{2,0,1:T(2,128)}), f32[2,32,512]{2,0,1:T(2,128)S(1)}, u32[]{:S(2)}, u32[]{:S(2)}) %all-to-all-start) | async-done | bytes 131104 | tf_op jit(solution)/shard_map/all_to_all | solution.py:348
  37.9 0.7 copy.13.arrived_ref
  38.5 12.3 %inject.1.inj = f32[64,1024]{1,0:T(8,128)} custom-call(f32[2,32,512]{2,1,0:T(8,128)} %copy.13.arrived_ref, f32[64,64]{1,0:T(8,128)} %wave_ref.1), custom_call_target="tpu_custom_call" | custom-call | tf_op jit(solution)/shard_map/inject/pallas_call | solution.py:107
  50.8 0.0 copy-start
  50.8 0.9 copy-done
  51.8 122.6 %grid.1 = (f32[32,4096]{1,0:T(8,128)S(1)}, f32[32,4096]{1,0:T(8,128)S(1)}) custom-call(f32[32,4096]{1,0:T(8,128)S(1)} %bitcast.32, f32[64,1024]{1,0:T(8,128)S(1)} %copy-done, f32[8,32,128]{2,1,0:T(8,128)S(1)} %constant_dynamic-update-slice_fusion.coef), custom_call_target="tpu_custom_call" | custom-call | tf_op jit(solution)/shard_map/grid/pallas_call | solution.py:310
  174.3 0.9 copy.15
  175.2 0.9 copy.16
  (8 shorter events, 0.0 us)
Async XLA Ops:
  0.6 8.7 %copy-start.5 = (s32[8192,1]{0,1:T(1,128)S(1)}, s32[8192,1]{0,1:T(1,128)}, u32[]{:S(2)}) copy-start(s32[8192,1]{0,1:T(1,128)} %param.16) | copy-start | bytes 98308
  1.4 29.2 %collective-permute-start = (f32[4,1,128]{2,1,0:T(1,128)S(1)}, f32[4,1,128]{2,1,0:T(1,128)S(1)}, u32[]{:S(2)}, u32[]{:S(2)}) collective-permute-start(f32[4,1,128]{2,1,0:T(1,128)S(1)} %slice.15), channel_id=1, source_target_pairs={{0,4},{4,8},{8,12},{12,16},{16,20},{20,24},{24,28},{1,5},{5,9},{9,... | collective-permute-start | bytes 6152 | tf_op jit(solution)/shard_map/ppermute | solution.py:338
  4.6 26.0 %collective-permute-start.1 = (f32[4,8,1]{2,1,0:T(8,128)S(1)}, f32[4,8,1]{2,1,0:T(8,128)S(1)}, u32[]{:S(2)}, u32[]{:S(2)}) collective-permute-start(f32[4,8,1]{2,1,0:T(8,128)S(1)} %slice.17), channel_id=1, source_target_pairs={{0,1},{1,2},{2,3},{4,5},{5,6},{6,7},{8,9},{9,10},{10,11},{12,13},{... | collective-permute-start | bytes 392 | tf_op jit(solution)/shard_map/ppermute | solution.py:338
  10.1 0.8 copy-start.6
  10.9 0.8 copy-start.7
  11.6 0.8 copy-start.8
  13.0 17.2 %copy-start.1 = (f32[32,4,8,128]{3,2,1,0:T(8,128)S(1)}, f32[32,4,8,128]{3,2,1,0:T(8,128)}, u32[]{:S(2)}) copy-start(f32[32,4,8,128]{3,2,1,0:T(8,128)} %param.10) | copy-start | bytes 1572868
  24.5 13.4 %all-to-all-start = ((f32[2,32,512]{2,0,1:T(2,128)}), f32[2,32,512]{2,0,1:T(2,128)S(1)}, u32[]{:S(2)}, u32[]{:S(2)}) async-start(f32[2,32,512]{2,0,1:T(2,128)} %copy.12), calls=%async_computation | async-start | bytes 262144 | tf_op jit(solution)/shard_map/all_to_all | solution.py:348
  29.5 0.7 copy-start.4
  30.2 0.7 copy-start.2
  30.2 0.7 copy-start.3
  30.2 0.7 copy-start.9
  50.8 0.9 copy-start
where the time goes:
time: 177 us; the launch traced here: 176 us
  Pallas kernels  145 us (82%)
  starting transfers between devices  11.7 us (7%)
  local copies, waits for them, and re-layouts  11.4 us (6%)
  waiting for transfers between devices  6.64 us (4%)
    pallas_call x1, Pallas kernels, solve_grid(): pl.pallas_call(functools.partial(grid_kernel, nx, ny, steps, layers, tile...  123 us
    pallas_call x1, Pallas kernels, inject(): pl.pallas_call(functools.partial(inject_kernel, parts), out_shape=jax.Sha...  12.3 us
    pallas_call x1, Pallas kernels, bin_instances(): pl.pallas_call(functools.partial(bin_kernel, devices, capacity), out_shap...  9.78 us
    ppermute x2, starting transfers between devices, shifted(): return lax.ppermute(x, axis, [(i, i + 1) for i in range(length - 1)])  6.67 us
    all_to_all x1, waiting for transfers between devices, body(): lax.all_to_all(slots.reshape(2, devices, capacity), ('gx', 'gy'), split_a...  6.63 us
    unnamed x26, local copies, waits for them, and re-layouts  5.07 us
    all_to_all x1, starting transfers between devices, body(): lax.all_to_all(slots.reshape(2, devices, capacity), ('gx', 'gy'), split_a...  5.02 us
  transfers between devices with their start and end apart: 3, of which 1 were waited for; matrix products, arithmetic and copies ran while one was open for 4% of the time, Pallas kernels for 6%

commit v1 on v0

v1 whole, which is shorter than its diff:
```python
import functools

import jax
import jax.numpy as jnp
from jax import lax
from jax.experimental import pallas as pl
from jax.experimental.pallas import tpu as pltpu
from jax.sharding import PartitionSpec as P

ITERS = 3
SUBLANES = 8
SCALE = 6.0
SHIFT = 1.125
LANES = 128
MESH = pl.DeviceIdType.MESH
NT = (((1,), (1,)), ((), ()))
F32 = jnp.float32
BF16 = jnp.bfloat16


def split3(x):
    first = x.astype(BF16).astype(F32)
    rest = x - first
    second = rest.astype(BF16).astype(F32)
    return first, second, rest - second


def rows_iota(rows, cols):
    return lax.broadcasted_iota(jnp.int32, (rows, cols), 0)


def bin_kernel(devices, capacity, target_ref, cell_ref, wave_ref, amp_ref, out_ref, acc_ref):
    blocks, width = target_ref.shape
    rows = out_ref.shape[1]
    before = (
        rows_iota(width, width) < lax.broadcasted_iota(jnp.int32, (width, width), 1)
    ).astype(F32).astype(BF16)
    acc_ref[...] = jnp.zeros_like(acc_ref)

    def step(b, base):
        target = target_ref[pl.ds(b, 1), :]
        hits = (rows_iota(devices, width) == target).astype(F32)
        ahead = jnp.dot(hits.astype(BF16), before, preferred_element_type=F32)
        position = jnp.sum(hits * (ahead + base), axis=0, keepdims=True)
        slot = target * capacity + position.astype(jnp.int32)
        row_hits = rows_iota(rows, width) == (slot >> 7)
        lane_hits = (rows_iota(LANES, width) == (slot & 127)).astype(F32).astype(BF16)
        code = cell_ref[pl.ds(b, 1), :] * 64 + wave_ref[pl.ds(b, 1), :]
        parts = split3(amp_ref[pl.ds(b, 1), :]) + (
            (code >> 8).astype(F32),
            (code & 255).astype(F32),
        )
        for i, part in enumerate(parts):
            left = jnp.where(row_hits, part, 0.0).astype(BF16)
            acc_ref[i] += lax.dot_general(left, lane_hits, NT, preferred_element_type=F32)
        return base + jnp.sum(hits, axis=1, keepdims=True)

    lax.fori_loop(0, blocks, step, jnp.zeros((devices, 1), F32), unroll=2)
    out_ref[0] = (acc_ref[2] + acc_ref[1]) + acc_ref[0]
    out_ref[1] = acc_ref[3] * 256.0 + acc_ref[4]


def bin_instances(devices, capacity, target, cells, wave_ids, amps):
    width = 512
    shape = (target.shape[0] // width, width)
    rows = devices * capacity // LANES
    return pl.pallas_call(
        functools.partial(bin_kernel, devices, capacity),
        out_shape=jax.ShapeDtypeStruct((2, rows, LANES), F32),
        in_specs=[pl.BlockSpec(memory_space=pltpu.VMEM)] * 4,
        out_specs=pl.BlockSpec(memory_space=pltpu.VMEM),
        scratch_shapes=[pltpu.VMEM((5, rows, LANES), F32)],
        name="bin",
    )(*[x.reshape(shape) for x in (target, cells, wave_ids, amps)])


def inject_kernel(parts, arrived_ref, wave_ref, out_ref, acc_ref):
    sources, width = arrived_ref.shape[1:]
    kinds = wave_ref.shape[1]
    outs = wave_ref.shape[0]
    low_count = out_ref.shape[1] // parts
    table = jnp.concatenate(split3(wave_ref[...]), axis=0).astype(BF16)
    acc_ref[...] = jnp.zeros_like(acc_ref)

    def step(i, carry):
        amp = arrived_ref[0, pl.ds(i, 1), :]
        code = arrived_ref[1, pl.ds(i, 1), :].astype(jnp.int32)
        cell = code >> 6
        low, high = cell % low_count, cell // low_count
        kind_hits = (rows_iota(kinds, width) == (code & 63)).astype(F32).astype(BF16)
        picked = jnp.dot(table, kind_hits, preferred_element_type=F32)
        wave = (picked[2 * outs :] + picked[outs : 2 * outs]) + picked[:outs]
        currents = (wave * amp).astype(BF16).astype(F32)
        low_hits = (rows_iota(low_count, width) == low).astype(F32).astype(BF16)
        left = jnp.concatenate(
            [jnp.where(high == h, currents, 0.0).astype(BF16) for h in range(parts)], axis=0
        )
        acc_ref[...] += lax.dot_general(left, low_hits, NT, preferred_element_type=F32)
        return carry

    lax.fori_loop(0, sources, step, 0, unroll=2)
    for h in range(parts):
        out_ref[:, h * low_count : (h + 1) * low_count] = acc_ref[h * outs : (h + 1) * outs]


def inject(arrived, waveforms, die_cells):
    parts = 4
    return pl.pallas_call(
        functools.partial(inject_kernel, parts),
        out_shape=jax.ShapeDtypeStruct((waveforms.shape[0], die_cells), F32),
        in_specs=[pl.BlockSpec(memory_space=pltpu.VMEM)] * 2,
        out_specs=pl.BlockSpec(memory_space=pltpu.VMEM),
        scratch_shapes=[pltpu.VMEM((parts * waveforms.shape[0], die_cells // parts), F32)],
        name="inject",
    )(arrived, waveforms)


def across(tile, k):
    return jnp.broadcast_to(tile[:, k : k + 1], tile.shape)


def down(tile, a):
    return jnp.broadcast_to(tile[a : a + 1, :], tile.shape)


def eliminate_panel(tiles, p):
    tile, k = tiles[p], SUBLANES * p
    sub = rows_iota(SUBLANES, LANES)
    columns = [across(tile, k + b) for b in range(SUBLANES)]
    pivot = [[down(columns[b], a) for b in range(SUBLANES)] for a in range(SUBLANES)]
    right = [down(tile, a) for a in range(SUBLANES)]
    inverse = []
    for a in range(SUBLANES):
        inverse.append(1.0 / pivot[a][a])
        for b in range(a + 1, SUBLANES):
            factor = pivot[a][b] * inverse[a]
            right[b] = right[b] - factor * right[a]
            for c in range(b, SUBLANES):
                pivot[b][c] = pivot[b][c] - factor * pivot[a][c]
    solved = [None] * SUBLANES
    for a in reversed(range(SUBLANES)):
        row = right[a]
        for b in reversed(range(a + 1, SUBLANES)):
            row = row - pivot[a][b] * solved[b]
        solved[a] = row * inverse[a]
    fresh = []
    for i, other in enumerate(tiles):
        if i == p:
            result = solved[0]
            for a in range(1, SUBLANES):
                result = jnp.where(sub == a, solved[a], result)
        else:
            result = other
            for b in range(SUBLANES):
                result = result - across(other, k + b) * solved[b]
        fresh.append(result)
    return fresh


def halves(x):
    high = x.astype(BF16)
    return high, (x - high.astype(F32)).astype(BF16)


def grid_kernel(
    nx, ny, steps, layers, tile_x,
    v_in, inj, coef, v, r,
    k0, k1, k2, basis, xl, ys, yl, gl, hl,
    xsend, xrecv, ysend, yrecv, gsend, grecv, hsend, hrecv,
):
    gx, gy = lax.axis_index("gx"), lax.axis_index("gy")
    size = v.shape[2]
    count = layers * tile_x
    halos = 1 + ITERS * steps
    packed = LANES // size
    part = size // packed
    spans = ((0, 3 * part), (3 * part, 2 * part), (5 * part, part))
    lane = lax.broadcasted_iota(jnp.int32, (size, LANES), 1)
    group = lax.broadcasted_iota(jnp.int32, (part, LANES), 1) // size
    edges = [l * tile_x + x for l in range(layers) for x in (0, tile_x - 1)]
    inner = [c for c in range(count) if c not in edges]
    fields = (k0, k1, k2)

    def at(ref, c):
        return ref.at[c // tile_x, c % tile_x]

    def x_copies(src, e):
        return [
            pltpu.make_async_remote_copy(
                src.at[:, tile_x - 1 if side == 0 else 0], xl.at[e, side],
                xsend.at[e, side], xrecv.at[e, side],
                device_id={"gx": lax.rem(gx + (1 if side == 0 else nx - 1), nx)},
                device_id_type=MESH,
            )
            for side in range(2)
        ]

    def y_copies(e):
        return [
            pltpu.make_async_remote_copy(
                ys.at[e, side], yl.at[e, side], ysend.at[e, side], yrecv.at[e, side],
                device_id={"gy": lax.rem(gy + (1 if side == 0 else ny - 1), ny)},
                device_id_type=MESH,
            )
            for side in range(2)
        ]

    def start(copies, me, n):
        pl.when(me < n - 1)(copies[0].start)
        pl.when(me > 0)(copies[1].start)

    def finish(copies, me, n):
        @pl.when(me > 0)
        def _():
            copies[0].wait_recv()
            copies[1].wait_send()

        @pl.when(me < n - 1)
        def _():
            copies[1].wait_recv()
            copies[0].wait_send()

    def arrive(src, e):
        finish(x_copies(src, e), gx, nx)
        finish(y_copies(e), gy, ny)

    class Rim:
        def __init__(self):
            self.last = jnp.zeros((size, LANES), F32)
            self.first = self.last

        def add(self, c, f):
            self.last = jnp.where(lane == c, pltpu.roll(f, (c + 1) % LANES, 1), self.last)
            self.first = jnp.where(lane == c, pltpu.roll(f, c, 1) if c else f, self.first)

        def send(self, e):
            ys[e, 0] = self.last
            ys[e, 1] = self.first
            start(y_copies(e), gy, ny)

    def stencil(src, e, own, emit, after_edges):
        y_low, y_high = yl[e, 0], yl[e, 1]
        for n, c in enumerate(edges + inner):
            l, x = divmod(c, tile_x)
            f = src[l, x]

            def k(i):
                return coef[i, c : c + 1, :]

            high = src[l, x + 1] if x + 1 < tile_x else xl[e, 1, l]
            low = src[l, x - 1] if x else xl[e, 0, l]
            total = k(own) * f - k(2) * high - k(3) * low
            after = jnp.where(
                lane == LANES - 1, pltpu.roll(y_high, LANES - 1 - c, 1), pltpu.roll(f, LANES - 1, 1)
            )
            ahead = jnp.where(
                lane == 0, pltpu.roll(y_low, LANES - c, 1) if c else y_low, pltpu.roll(f, 1, 1)
            )
            total = total - k(4) * after - k(5) * ahead
            if l + 1 < layers:
                total = total - k(6) * src[l + 1, x]
            if l:
                total = total - k(7) * src[l - 1, x]
            emit(c, total)
            if n + 1 == len(edges):
                after_edges()

    def split(j, c, f):
        high, low = halves(f)
        cols = slice(c * LANES, (c + 1) * LANES)
        basis[j * size : (j + 1) * size, cols] = high
        basis[(ITERS + 1 + j) * size : (ITERS + 2 + j) * size, cols] = low

    def grams(left, j):
        def rows(i):
            return [basis[b * size : (b + 1) * size, :] for b in (i, ITERS + 1 + i)]

        every = [block for i in left for block in rows(i)]
        product = lax.dot_general(
            jnp.concatenate(every, axis=0), jnp.concatenate(rows(j), axis=0), NT,
            preferred_element_type=F32,
        )
        product = product[:, :size] + product[:, size:]
        return [
            product[2 * i * size : (2 * i + 1) * size] + product[(2 * i + 1) * size : (2 * i + 2) * size]
            for i in range(len(left))
        ]

    def pack(matrix):
        return jnp.concatenate([matrix[i * part : (i + 1) * part] for i in range(packed)], axis=1)

    def gather(land, step, g, ssem, rsem, axis, me, n):
        rows = pl.ds(spans[g][0], spans[g][1])
        return [
            pltpu.make_async_remote_copy(
                land.at[step, me, rows], land.at[step, me, rows],
                ssem.at[step, g, j], rsem.at[step, g, j],
                device_id={axis: lax.rem(me + j, n)}, device_id_type=MESH,
            )
            for j in range(1, n)
        ]

    def along_x(step, g):
        return gather(gl, step, g, gsend, grecv, "gx", gx, nx)

    def along_y(step, g):
        return gather(hl, step, g, hsend, hrecv, "gy", gy, ny)

    def add_start(step, g, matrices):
        for i, matrix in enumerate(matrices):
            gl[step, gx, pl.ds(spans[g][0] + i * part, part), :] = pack(matrix)
        for copy in along_x(step, g):
            copy.start()

    def landed(land, copies, step, g, n):
        for copy in copies:
            copy.wait()
        first, rows = spans[g]
        total = land[step, 0, first : first + rows, :]
        for j in range(1, n):
            total = total + land[step, j, first : first + rows, :]
        return total

    def add_turn(step, g):
        total = landed(gl, along_x(step, g), step, g, nx)
        hl[step, gy, pl.ds(*spans[g]), :] = total
        for copy in along_y(step, g):
            copy.start()

    def add_finish(step, g):
        total = landed(hl, along_y(step, g), step, g, ny)
        return [total[i * part : (i + 1) * part] for i in range(spans[g][1] // part)]

    def place(matrix, g, block):
        shift = ((block - g) * size) % LANES
        return pltpu.roll(matrix, shift, 1) if shift else matrix

    for e in range(halos):
        for me, n, land in ((gx, nx, xl), (gy, ny, yl)):
            for side, last in ((0, 0), (1, n - 1)):
                @pl.when(me == last)
                def _():
                    land[e, side] = jnp.zeros(land.shape[2:], F32)

    barrier = pltpu.get_barrier_semaphore()
    for axis, me, n in (("gx", gx, nx), ("gy", gy, ny)):
        for j in range(1, n):
            pl.semaphore_signal(
                barrier, inc=1, device_id={axis: lax.rem(me + j, n)}, device_id_type=MESH
            )
    pl.semaphore_wait(barrier, nx + ny - 2)

    rim = Rim()
    for c in range(count):
        f = v_in[pl.ds(c, size, stride=count), :]
        v[c // tile_x, c % tile_x] = f
        rim.add(c, f)
    start(x_copies(v, 0), gx, nx)
    rim.send(0)
    arrive(v, 0)
    rim = Rim()

    def first_residual(c, total):
        f = -SCALE * total
        if c < tile_x:
            f = f - inj[:size, c * LANES : (c + 1) * LANES]
        k0[c // tile_x, c % tile_x] = f
        r[c // tile_x, c % tile_x] = f
        rim.add(c, f)

    stencil(v, 0, 1, first_residual, lambda: start(x_copies(k0, 1), gx, nx))
    rim.send(1)

    def time_step(step, carry):
        e = 1 + ITERS * step
        for c in range(count):
            split(0, c, k0[c // tile_x, c % tile_x])
        moments = grams([0], 0)
        for j in range(1, ITERS + 1):
            arrive(fields[j - 1], e + j - 1)
            if j > 1:
                add_turn(step, j - 2)
            rim = Rim()

            def next_field(c, total):
                split(j, c, total)
                if j < ITERS:
                    fields[j][c // tile_x, c % tile_x] = total
                    rim.add(c, total)

            def send_edges():
                if j < ITERS:
                    start(x_copies(fields[j], e + j), gx, nx)

            stencil(fields[j - 1], e + j - 1, 0, next_field, send_edges)
            if j < ITERS:
                rim.send(e + j)
            moments = moments + grams([j - 1, j] if j < ITERS else [j - 1], j)
            add_start(step, j - 1, moments)
            moments = []
        m = add_finish(step, 0)
        add_turn(step, ITERS - 1)
        m = m + add_finish(step, 1)
        m.append(jnp.zeros_like(m[0]))
        shifted_m = [SCALE * (m[i + 1] + SHIFT * m[i]) for i in range(len(m) - 1)]
        tiles = []
        for i in range(ITERS):
            for g in range(packed):
                tile = place(m[i], g, ITERS)
                for block in range(ITERS):
                    tile = jnp.where(group == block, place(shifted_m[i + block], g, block), tile)
                tiles.append(tile)
        early = (ITERS - 1) * packed
        for p in range(early):
            tiles = eliminate_panel(tiles, p)
        (final,) = add_finish(step, ITERS - 1)
        for g in range(packed):
            at_end = jnp.where(group == ITERS - 1, SCALE * place(final, g, ITERS - 1), 0.0)
            tiles[early + g] = tiles[early + g] + at_end
        for p in range(early, ITERS * packed):
            tiles = eliminate_panel(tiles, p)
        solved = jnp.concatenate(tiles, axis=0)[:, ITERS * size : (ITERS + 1) * size]
        none = jnp.zeros((size, size), F32)
        take = jnp.concatenate([solved, none], axis=0)
        drop = jnp.concatenate([none, solved], axis=0)
        both = jnp.concatenate([take, -SCALE * (drop + SHIFT * take)], axis=1)
        high, low = halves(both)
        turned = jnp.concatenate([high.astype(F32), low.astype(F32)], axis=1).T.astype(BF16)
        turned = jnp.concatenate([turned, turned], axis=1)
        more = step + 1 < steps
        rim = Rim()
        pairs = sorted({c - c % 2 for c in edges})
        for n, c in enumerate(pairs + [c for c in range(0, count, 2) if c not in pairs]):
            out = jnp.dot(
                turned, basis[:, c * LANES : (c + 2) * LANES], preferred_element_type=F32
            )
            out = out[: 2 * size] + out[2 * size :]
            for i in range(2):
                l, x = divmod(c + i, tile_x)
                cols = slice(i * LANES, (i + 1) * LANES)
                change = out[:size, cols]
                v[l, x] = v[l, x] + change
                left = k0[l, x] + out[size:, cols]
                r[l, x] = left
                left = left + coef[8, c + i : c + i + 1, :] * change
                if c + i < tile_x:
                    after = jnp.minimum(step + 1, steps - 1)
                    here = slice((c + i) * LANES, (c + i + 1) * LANES)
                    left = left - (
                        inj[pl.ds(pl.multiple_of(after * size, size), size), here]
                        - inj[pl.ds(pl.multiple_of(step * size, size), size), here]
                    )
                k0[l, x] = left
                rim.add(c + i, left)
            if n + 1 == len(pairs):
                @pl.when(more)
                def _():
                    start(x_copies(k0, e + ITERS), gx, nx)

        @pl.when(more)
        def _():
            rim.send(e + ITERS)

        return carry

    lax.fori_loop(0, steps, time_step, 0)


def solve_grid(nx, ny, steps, layers, tile_x, volts, injected, coef):
    size = injected.shape[0] // steps
    halos = 1 + steps * ITERS
    packed = (2 * ITERS) * size * size // LANES
    field = (layers, tile_x, size, LANES)
    dma = pltpu.SemaphoreType.DMA
    return pl.pallas_call(
        functools.partial(grid_kernel, nx, ny, steps, layers, tile_x),
        out_shape=[jax.ShapeDtypeStruct(field, F32)] * 2,
        in_specs=[pl.BlockSpec(memory_space=pltpu.VMEM)] * 3,
        out_specs=[pl.BlockSpec(memory_space=pltpu.VMEM)] * 2,
        scratch_shapes=[
            pltpu.VMEM(field, F32),
            pltpu.VMEM(field, F32),
            pltpu.VMEM(field, F32),
            pltpu.VMEM((2 * (ITERS + 1) * size, layers * tile_x * LANES), BF16),
            pltpu.VMEM((halos, 2, layers, size, LANES), F32),
            pltpu.VMEM((halos, 2, size, LANES), F32),
            pltpu.VMEM((halos, 2, size, LANES), F32),
            pltpu.VMEM((steps, nx, packed, LANES), F32),
            pltpu.VMEM((steps, ny, packed, LANES), F32),
            dma((halos, 2)), dma((halos, 2)), dma((halos, 2)), dma((halos, 2)),
            dma((steps, ITERS, nx)), dma((steps, ITERS, nx)),
            dma((steps, ITERS, ny)), dma((steps, ITERS, ny)),
        ],
        compiler_params=pltpu.CompilerParams(
            collective_id=0, has_side_effects=True, vmem_limit_bytes=48 * 1024 * 1024
        ),
        name="grid",
    )(volts, injected, coef)


def shifted(x, axis):
    length = lax.axis_size(axis)
    return lax.ppermute(x, axis, [(i, i + 1) for i in range(length - 1)])


def body(volts, cap, cond_x, cond_y, via, waveforms, placement, cells, wave_ids, amps):
    nx, ny = lax.axis_size("gx"), lax.axis_size("gy")
    devices = nx * ny
    scenarios, layers, tile_x, tile_y = volts.shape
    steps = waveforms.shape[0] // scenarios
    capacity = 2 * cells.shape[0] // devices
    slots = bin_instances(devices, capacity, placement[:, 0], cells, wave_ids, amps)
    arrived = lax.all_to_all(
        slots.reshape(2, devices, capacity), ("gx", "gy"), split_axis=1, concat_axis=1, tiled=True
    )
    injected = inject(arrived, waveforms, tile_x * tile_y)
    rim_x = shifted(cond_x[:, -1:, :], "gx")
    rim_y = shifted(cond_y[:, :, -1:], "gy")
    x_low = jnp.concatenate([rim_x, cond_x[:, :-1, :]], axis=1)
    y_low = jnp.concatenate([rim_y, cond_y[:, :, :-1]], axis=2)
    via_low = jnp.concatenate([jnp.zeros_like(via[:1]), via[:-1]], axis=0)
    at_x = lax.broadcasted_iota(jnp.int32, cond_x.shape, 1) + lax.axis_index("gx") * tile_x
    at_y = lax.broadcasted_iota(jnp.int32, cond_y.shape, 2) + lax.axis_index("gy") * tile_y
    x_next = jnp.where(at_x == nx * tile_x - 1, 0.0, cond_x)
    y_next = jnp.where(at_y == ny * tile_y - 1, 0.0, cond_y)
    around = cond_x + x_low + cond_y + y_low + via + via_low
    coef = jnp.stack([cap + around, around, x_next, x_low, y_next, y_low, via, via_low]) / SCALE
    coef = jnp.concatenate([coef[:1] - SHIFT, coef[1:], cap[None]], axis=0)
    coef = coef.reshape(9, layers * tile_x, tile_y)
    out, residual = solve_grid(
        nx, ny, steps, layers, tile_x, volts.reshape(-1, tile_y), injected, coef
    )
    return out.transpose(2, 0, 1, 3), residual.transpose(2, 0, 1, 3)


def solution(mesh):
    grid = P(None, "gx", "gy")
    field = P(None, None, "gx", "gy")
    flat = P(("gx", "gy"))
    return jax.shard_map(
        body,
        mesh=mesh,
        in_specs=(field, grid, grid, grid, grid, P(), P(("gx", "gy"), None), flat, flat, flat),
        out_specs=(field, field),
        check_vma=False,
    )
```

time: 177 us -> 110 us (0.62)
  Pallas kernels: 145 us -> 76.9 us
    pallas_call x1, Pallas kernels: 123 us -> 54.8 us  [solve_grid(): pl.pallas_call(functools.partial(grid_kernel, nx, ny, steps, layers, tile...]
    unnamed x26 -> x25, local copies, waits for them, and re-layouts: 5.07 us -> 4.77 us
  transfers between devices with their start and end apart: 3 -> 3, of which waited for: 1 -> 1; matrix products, arithmetic and copies ran while one was open for 4% -> 6% of each run, Pallas kernels for 6% -> 9%
where the time goes in v1:
time: 110 us; the launch traced here: 109 us
  Pallas kernels  76.9 us (70%)
  starting transfers between devices  11.7 us (11%)
  local copies, waits for them, and re-layouts  11.1 us (10%)
  waiting for transfers between devices  7.28 us (7%)
    pallas_call x1, Pallas kernels, solve_grid(): pl.pallas_call(functools.partial(grid_kernel, nx, ny, steps, layers, tile...  54.8 us
    pallas_call x1, Pallas kernels, inject(): pl.pallas_call(functools.partial(inject_kernel, parts), out_shape=jax.Sha...  12.3 us
    pallas_call x1, Pallas kernels, bin_instances(): pl.pallas_call(functools.partial(bin_kernel, devices, capacity), out_shap...  9.73 us
    all_to_all x1, waiting for transfers between devices, body(): lax.all_to_all(slots.reshape(2, devices, capacity), ('gx', 'gy'), split_a...  7.28 us
    ppermute x2, starting transfers between devices, shifted(): return lax.ppermute(x, axis, [(i, i + 1) for i in range(length - 1)])  6.67 us
    all_to_all x1, starting transfers between devices, body(): lax.all_to_all(slots.reshape(2, devices, capacity), ('gx', 'gy'), split_a...  5.02 us
    unnamed x25, local copies, waits for them, and re-layouts  4.77 us
  transfers between devices with their start and end apart: 3, of which 1 were waited for; matrix products, arithmetic and copies ran while one was open for 6% of the time, Pallas kernels for 9%

profile of v1, /device:TPU:0, one launch (start us, length us, event | category | flops | bytes accessed | tf_op | source)
XLA Modules:
  0.0 108.8 jit_solution(16693504274567108433)
XLA Ops:
  0.6 0.0 copy-start.6
  0.6 0.7 slice.21
  1.4 2.4 %collective-permute-start = (f32[4,1,128]{2,1,0:T(1,128)S(1)}, f32[4,1,128]{2,1,0:T(1,128)S(1)}, u32[]{:S(2)}, u32[]{:S(2)}) collective-permute-start(f32[4,1,128]{2,1,0:T(1,128)S(1)} %slice.21), channel_id=1, source_target_pairs={{0,4},{4,8},{8,12},{12,16},{16,20},{20,24},{24,28},{1,5},{5,9},{9,... | collective-permute-start | bytes 6152 | tf_op jit(solution)/shard_map/ppermute | solution.py:503
  3.8 0.8 slice.23
  4.6 4.3 %collective-permute-start.1 = (f32[4,8,1]{2,1,0:T(8,128)S(1)}, f32[4,8,1]{2,1,0:T(8,128)S(1)}, u32[]{:S(2)}, u32[]{:S(2)}) collective-permute-start(f32[4,8,1]{2,1,0:T(8,128)S(1)} %slice.23), channel_id=1, source_target_pairs={{0,1},{1,2},{2,3},{4,5},{5,6},{6,7},{8,9},{9,10},{10,11},{12,13},{... | collective-permute-start | bytes 392 | tf_op jit(solution)/shard_map/ppermute | solution.py:503
  8.8 0.5 broadcast.19
  9.4 0.0 copy-done.6
  9.4 0.7 reduce.3
  10.1 0.0 copy-start.7
  10.1 0.6 reshape_squeeze.3.target_ref
  10.7 0.1 copy-done.7
  10.9 0.0 copy-start.8
  10.9 0.6 reshape.25.cell_ref
  11.5 0.1 copy-done.8
  11.6 0.0 copy-start.9
  11.6 0.6 reshape.26.wave_ref
  12.2 0.2 copy-done.9
  12.4 0.6 reshape.27.amp_ref
  13.0 9.7 %bin.1 = f32[2,128,128]{2,1,0:T(8,128)} custom-call(s32[16,512]{1,0:T(8,128)} %reshape_squeeze.3.target_ref, s32[16,512]{1,0:T(8,128)} %reshape.25.cell_ref, s32[16,512]{1,0:T(8,128)} %reshape.26.wave_ref, f32[16,512]{1,0:T(8,128)} %reshape.27.amp_ref), custom_call_target="tpu_custom_call" | custom-call | tf_op jit(solution)/shard_map/bin/pallas_call | solution.py:67
  22.7 0.9 reshape.28
  23.6 0.8 copy.14
  24.4 0.0 copy-start.4
  24.4 0.0 copy-start.5
  24.4 5.0 %all-to-all-start = ((f32[2,32,512]{2,0,1:T(2,128)}), f32[2,32,512]{2,0,1:T(2,128)S(1)}, u32[]{:S(2)}, u32[]{:S(2)}) async-start(f32[2,32,512]{2,0,1:T(2,128)} %copy.14), calls=%async_computation | async-start | bytes 262144 | tf_op jit(solution)/shard_map/all_to_all | solution.py:513
  29.4 0.0 copy-start.3
  29.5 0.0 copy-start.2
  29.5 0.0 copy-done.4
  29.5 0.0 collective-permute-done.1
  29.5 0.0 collective-permute-done
  29.5 0.0 copy-done.5
  29.5 0.6 copy-done.3
  30.2 0.0 copy-done.2
  30.2 0.1 constant_dynamic-update-slice_fusion.7
  30.3 0.1 constant_dynamic-update-slice_fusion.5
  30.4 0.1 constant_dynamic-update-slice_fusion.2
  30.5 0.0 copy-start.1
  30.5 7.3 %all-to-all-done = f32[2,32,512]{2,0,1:T(2,128)S(1)} async-done(((f32[2,32,512]{2,0,1:T(2,128)}), f32[2,32,512]{2,0,1:T(2,128)S(1)}, u32[]{:S(2)}, u32[]{:S(2)}) %all-to-all-start) | async-done | bytes 131104 | tf_op jit(solution)/shard_map/all_to_all | solution.py:513
  37.8 0.7 copy.15.arrived_ref
  38.5 12.3 %inject.1.inj = f32[64,1024]{1,0:T(8,128)} custom-call(f32[2,32,512]{2,1,0:T(8,128)} %copy.15.arrived_ref, f32[64,64]{1,0:T(8,128)} %wave_ref.1), custom_call_target="tpu_custom_call" | custom-call | tf_op jit(solution)/shard_map/inject/pallas_call | solution.py:108
  50.8 0.0 copy-done.1
  50.8 0.0 copy-start
  50.8 0.9 copy-done
  51.7 54.8 %grid.1 = (f32[4,8,32,128]{3,2,1,0:T(8,128)S(1)}, f32[4,8,32,128]{3,2,1,0:T(8,128)S(1)}) custom-call(f32[1024,128]{1,0:T(8,128)S(1)} %bitcast.29, f32[64,1024]{1,0:T(8,128)S(1)} %copy-done, f32[9,32,128]{2,1,0:T(8,128)S(1)} %pad_maximum_fusion.coef), custom_call_target="tpu_custom_call" | custom-call | tf_op jit(solution)/shard_map/grid/pallas_call | solution.py:475
  106.6 1.1 %copy.16 = f32[32,4,8,128]{3,2,1,0:T(8,128)} copy(f32[32,4,8,128]{3,0,2,1:T(8,128)S(1)} %bitcast.31) | data formatting | bytes 1048576
  107.7 1.1 %copy.17 = f32[32,4,8,128]{3,2,1,0:T(8,128)} copy(f32[32,4,8,128]{3,0,2,1:T(8,128)S(1)} %bitcast.30) | data formatting | bytes 1048576
  (12 shorter events, 0.1 us)
Async XLA Ops:
  0.6 8.7 %copy-start.6 = (s32[8192,1]{0,1:T(1,128)S(1)}, s32[8192,1]{0,1:T(1,128)}, u32[]{:S(2)}) copy-start(s32[8192,1]{0,1:T(1,128)} %param.16) | copy-start | bytes 98308
  1.4 28.2 %collective-permute-start = (f32[4,1,128]{2,1,0:T(1,128)S(1)}, f32[4,1,128]{2,1,0:T(1,128)S(1)}, u32[]{:S(2)}, u32[]{:S(2)}) collective-permute-start(f32[4,1,128]{2,1,0:T(1,128)S(1)} %slice.21), channel_id=1, source_target_pairs={{0,4},{4,8},{8,12},{12,16},{16,20},{20,24},{24,28},{1,5},{5,9},{9,... | collective-permute-start | bytes 6152 | tf_op jit(solution)/shard_map/ppermute | solution.py:503
  4.6 25.0 %collective-permute-start.1 = (f32[4,8,1]{2,1,0:T(8,128)S(1)}, f32[4,8,1]{2,1,0:T(8,128)S(1)}, u32[]{:S(2)}, u32[]{:S(2)}) collective-permute-start(f32[4,8,1]{2,1,0:T(8,128)S(1)} %slice.23), channel_id=1, source_target_pairs={{0,1},{1,2},{2,3},{4,5},{5,6},{6,7},{8,9},{9,10},{10,11},{12,13},{... | collective-permute-start | bytes 392 | tf_op jit(solution)/shard_map/ppermute | solution.py:503
  10.1 0.8 copy-start.7
  10.9 0.8 copy-start.8
  11.6 0.8 copy-start.9
  24.4 5.1 %copy-start.4 = (f32[4,8,128]{2,1,0:T(8,128)S(1)}, f32[4,8,128]{2,1,0:T(8,128)}, u32[]{:S(2)}) copy-start(f32[4,8,128]{2,1,0:T(8,128)} %param.14) | copy-start | bytes 49156
  24.4 5.1 %copy-start.5 = (f32[4,8,128]{2,1,0:T(8,128)S(1)}, f32[4,8,128]{2,1,0:T(8,128)}, u32[]{:S(2)}) copy-start(f32[4,8,128]{2,1,0:T(8,128)} %param.11) | copy-start | bytes 49156
  24.4 13.4 %all-to-all-start = ((f32[2,32,512]{2,0,1:T(2,128)}), f32[2,32,512]{2,0,1:T(2,128)S(1)}, u32[]{:S(2)}, u32[]{:S(2)}) async-start(f32[2,32,512]{2,0,1:T(2,128)} %copy.14), calls=%async_computation | async-start | bytes 262144 | tf_op jit(solution)/shard_map/all_to_all | solution.py:513
  29.4 0.7 copy-start.3
  29.5 0.7 copy-start.2
  30.5 20.3 %copy-start.1 = (f32[32,4,8,128]{3,2,1,0:T(8,128)S(1)}, f32[32,4,8,128]{3,2,1,0:T(8,128)}, u32[]{:S(2)}) copy-start(f32[32,4,8,128]{3,2,1,0:T(8,128)} %param.10) | copy-start | bytes 1572868
  50.8 1.0 copy-start

commit v2 on v1

--- a/solution.py
+++ b/solution.py
@@ -18,101 +18,16 @@
 BF16 = jnp.bfloat16
 
 
-def split3(x):
-    first = x.astype(BF16).astype(F32)
-    rest = x - first
-    second = rest.astype(BF16).astype(F32)
-    return first, second, rest - second
-
-
 def rows_iota(rows, cols):
     return lax.broadcasted_iota(jnp.int32, (rows, cols), 0)
 
 
-def bin_kernel(devices, capacity, target_ref, cell_ref, wave_ref, amp_ref, out_ref, acc_ref):
-    blocks, width = target_ref.shape
-    rows = out_ref.shape[1]
-    before = (
-        rows_iota(width, width) < lax.broadcasted_iota(jnp.int32, (width, width), 1)
-    ).astype(F32).astype(BF16)
-    acc_ref[...] = jnp.zeros_like(acc_ref)
-
-    def step(b, base):
-        target = target_ref[pl.ds(b, 1), :]
-        hits = (rows_iota(devices, width) == target).astype(F32)
-        ahead = jnp.dot(hits.astype(BF16), before, preferred_element_type=F32)
-        position = jnp.sum(hits * (ahead + base), axis=0, keepdims=True)
-        slot = target * capacity + position.astype(jnp.int32)
-        row_hits = rows_iota(rows, width) == (slot >> 7)
-        lane_hits = (rows_iota(LANES, width) == (slot & 127)).astype(F32).astype(BF16)
-        code = cell_ref[pl.ds(b, 1), :] * 64 + wave_ref[pl.ds(b, 1), :]
-        parts = split3(amp_ref[pl.ds(b, 1), :]) + (
-            (code >> 8).astype(F32),
-            (code & 255).astype(F32),
-        )
-        for i, part in enumerate(parts):
-            left = jnp.where(row_hits, part, 0.0).astype(BF16)
-            acc_ref[i] += lax.dot_general(left, lane_hits, NT, preferred_element_type=F32)
-        return base + jnp.sum(hits, axis=1, keepdims=True)
-
-    lax.fori_loop(0, blocks, step, jnp.zeros((devices, 1), F32), unroll=2)
-    out_ref[0] = (acc_ref[2] + acc_ref[1]) + acc_ref[0]
-    out_ref[1] = acc_ref[3] * 256.0 + acc_ref[4]
-
-
-def bin_instances(devices, capacity, target, cells, wave_ids, amps):
-    width = 512
-    shape = (target.shape[0] // width, width)
-    rows = devices * capacity // LANES
-    return pl.pallas_call(
-        functools.partial(bin_kernel, devices, capacity),
-        out_shape=jax.ShapeDtypeStruct((2, rows, LANES), F32),
-        in_specs=[pl.BlockSpec(memory_space=pltpu.VMEM)] * 4,
-        out_specs=pl.BlockSpec(memory_space=pltpu.VMEM),
-        scratch_shapes=[pltpu.VMEM((5, rows, LANES), F32)],
-        name="bin",
-    )(*[x.reshape(shape) for x in (target, cells, wave_ids, amps)])
-
-
-def inject_kernel(parts, arrived_ref, wave_ref, out_ref, acc_ref):
-    sources, width = arrived_ref.shape[1:]
-    kinds = wave_ref.shape[1]
-    outs = wave_ref.shape[0]
-    low_count = out_ref.shape[1] // parts
-    table = jnp.concatenate(split3(wave_ref[...]), axis=0).astype(BF16)
-    acc_ref[...] = jnp.zeros_like(acc_ref)
-
-    def step(i, carry):
-        amp = arrived_ref[0, pl.ds(i, 1), :]
-        code = arrived_ref[1, pl.ds(i, 1), :].astype(jnp.int32)
-        cell = code >> 6
-        low, high = cell % low_count, cell // low_count
-        kind_hits = (rows_iota(kinds, width) == (code & 63)).astype(F32).astype(BF16)
-        picked = jnp.dot(table, kind_hits, preferred_element_type=F32)
-        wave = (picked[2 * outs :] + picked[outs : 2 * outs]) + picked[:outs]
-        currents = (wave * amp).astype(BF16).astype(F32)
-        low_hits = (rows_iota(low_count, width) == low).astype(F32).astype(BF16)
-        left = jnp.concatenate(
-            [jnp.where(high == h, currents, 0.0).astype(BF16) for h in range(parts)], axis=0
-        )
-        acc_ref[...] += lax.dot_general(left, low_hits, NT, preferred_element_type=F32)
-        return carry
-
-    lax.fori_loop(0, sources, step, 0, unroll=2)
-    for h in range(parts):
-        out_ref[:, h * low_count : (h + 1) * low_count] = acc_ref[h * outs : (h + 1) * outs]
-
-
-def inject(arrived, waveforms, die_cells):
-    parts = 4
-    return pl.pallas_call(
-        functools.partial(inject_kernel, parts),
-        out_shape=jax.ShapeDtypeStruct((waveforms.shape[0], die_cells), F32),
-        in_specs=[pl.BlockSpec(memory_space=pltpu.VMEM)] * 2,
-        out_specs=pl.BlockSpec(memory_space=pltpu.VMEM),
-        scratch_shapes=[pltpu.VMEM((parts * waveforms.shape[0], die_cells // parts), F32)],
-        name="inject",
-    )(arrived, waveforms)
+def ones(mask):
+    return mask.astype(F32).astype(BF16)
+
+
+def wide(ref, row, count):
+    return jnp.concatenate([ref[pl.ds(row + i, 1), :] for i in range(count)], axis=1)
 
 
 def across(tile, k):
@@ -163,13 +78,16 @@
 
 
 def grid_kernel(
-    nx, ny, steps, layers, tile_x,
-    v_in, inj, coef, v, r,
+    nx, ny, steps, layers, tile_x, capacity,
+    v_hbm, cap_hbm, x_hbm, y_hbm, via_hbm, waves_hbm, target_hbm, cells_hbm, kinds_hbm, amps_hbm,
+    v, r,
+    v_in, cap, cond_x, cond_y, via, waves, target, cells, kinds, amps, isem,
     k0, k1, k2, basis, xl, ys, yl, gl, hl,
-    xsend, xrecv, ysend, yrecv, gsend, grecv, hsend, hrecv,
+    coef, xc, yc, spots, bins, send, land, table, inj,
+    xsend, xrecv, ysend, yrecv, gsend, grecv, hsend, hrecv, csend, crecv, asend, arecv,
 ):
     gx, gy = lax.axis_index("gx"), lax.axis_index("gy")
-    size = v.shape[2]
+    size = xl.shape[3]
     count = layers * tile_x
     halos = 1 + ITERS * steps
     packed = LANES // size
@@ -180,6 +98,12 @@
     edges = [l * tile_x + x for l in range(layers) for x in (0, tile_x - 1)]
     inner = [c for c in range(count) if c not in edges]
     fields = (k0, k1, k2)
+    devices = nx * ny
+    low_count = inj.shape[2]
+    high_count = inj.shape[1] // size
+    kind_count = waves.shape[1]
+    lane_count = bins.shape[1]
+    rows_a_plane = capacity // LANES
 
     def at(ref, c):
         return ref.at[c // tile_x, c % tile_x]
@@ -335,47 +259,251 @@
         shift = ((block - g) * size) % LANES
         return pltpu.roll(matrix, shift, 1) if shift else matrix
 
+    def rim_copies():
+        return [
+            pltpu.make_async_remote_copy(
+                from_ref, to_ref, csend.at[i], crecv.at[i],
+                device_id={axis: lax.rem(me + 1, n)}, device_id_type=MESH,
+            )
+            for i, (from_ref, to_ref, axis, me, n) in enumerate(
+                ((cond_x, xc, "gx", gx, nx), (cond_y, yc, "gy", gy, ny))
+            )
+        ]
+
+    def coefficients():
+        row = rows_iota(tile_x, LANES)
+        col = lax.broadcasted_iota(jnp.int32, (tile_x, LANES), 1)
+        above = jnp.zeros((tile_x, LANES), F32)
+        for l in range(layers):
+            at = slice(l * tile_x, (l + 1) * tile_x)
+            x_low = jnp.where(row == 0, pltpu.roll(xc[at], 1, 0), pltpu.roll(cond_x[at], 1, 0))
+            y_low = jnp.where(col == 0, pltpu.roll(yc[at], 1, 1), pltpu.roll(cond_y[at], 1, 1))
+            x_end = jnp.logical_and(row == tile_x - 1, gx == nx - 1)
+            y_end = jnp.logical_and(col == LANES - 1, gy == ny - 1)
+            around = cond_x[at] + x_low + cond_y[at] + y_low + via[at] + above
+            values = [
+                (cap[at] + around) / SCALE - SHIFT, around / SCALE,
+                jnp.where(x_end, 0.0, cond_x[at]) / SCALE, x_low / SCALE,
+                jnp.where(y_end, 0.0, cond_y[at]) / SCALE, y_low / SCALE,
+                via[at] / SCALE, above / SCALE, cap[at],
+            ]
+            for i, value in enumerate(values):
+                coef[i, at] = value
+            above = via[at]
+
+    def find_spots():
+        width = 2 * LANES
+        before = ones(rows_iota(width, width) < lax.broadcasted_iota(jnp.int32, (width, width), 1))
+        together = 4
+
+        def body(q, base):
+            hits = [
+                (rows_iota(devices, width) == wide(target, (q * together + i) * 2, 2)).astype(F32)
+                for i in range(together)
+            ]
+            ahead = jnp.dot(
+                jnp.concatenate(hits, axis=0).astype(BF16), before, preferred_element_type=F32
+            )
+            for i, hit in enumerate(hits):
+                count = ahead[i * devices : (i + 1) * devices]
+                spot = jnp.sum(hit * (count + base), axis=0, keepdims=True).astype(jnp.int32)
+                for half in range(2):
+                    at = pl.ds((q * together + i) * 2 + half, 1)
+                    spots[at, :] = spot[:, half * LANES : (half + 1) * LANES]
+                base = base + jnp.broadcast_to((count + hit)[:, width - 1 :], base.shape)
+            return base
+
+        lax.fori_loop(
+            0, target.shape[0] // (2 * together), body, jnp.zeros((devices, width), F32)
+        )
+
+    def fill_bins():
+        rows = bins.shape[0] // 4
+        width = 4 * LANES
+        bins[...] = jnp.zeros_like(bins)
+
+        def body(b, carry):
+            spot = wide(spots, b * 4, 4)
+            key = wide(target, b * 4, 4) + (spot // lane_count) * devices
+            mask = rows_iota(rows, width) == key
+            there = ones(rows_iota(lane_count, width) == spot % lane_count)
+            code = wide(cells, b * 4, 4) * kind_count + wide(kinds, b * 4, 4)
+            amp = wide(amps, b * 4, 4)
+            amp_high = amp.astype(BF16).astype(F32)
+            parts = (amp_high, amp - amp_high, (code >> 8).astype(F32), (code & 255).astype(F32))
+            left = jnp.concatenate([jnp.where(mask, p, 0.0).astype(BF16) for p in parts], axis=0)
+            bins[...] += lax.dot_general(left, there, NT, preferred_element_type=F32)
+            return carry
+
+        lax.fori_loop(0, target.shape[0] // 4, body, 0, unroll=2)
+        planes = (
+            bins[:rows] + bins[rows : 2 * rows],
+            bins[2 * rows : 3 * rows] * 256.0 + bins[3 * rows :],
+        )
+        if 2 * rows_a_plane < SUBLANES:
+            send[...] = jnp.zeros_like(send)
+        for i, plane in enumerate(planes):
+            for row in range(rows_a_plane):
+                first, col = divmod(row * LANES, lane_count)
+                send[pl.ds(i * rows_a_plane + row, devices, stride=SUBLANES), :] = plane[
+                    first * devices : (first + 1) * devices, col : col + LANES
+                ]
+
+    def bin_copy(j):
+        to_x = lax.rem(gx + j // ny, nx)
+        to_y = lax.rem(gy + j % ny, ny)
+        at = pl.multiple_of((to_x * ny + to_y) * SUBLANES, SUBLANES)
+        return pltpu.make_async_remote_copy(
+            send.at[pl.ds(at, SUBLANES)], land.at[j], asend.at[j], arecv.at[j],
+            device_id={"gx": to_x, "gy": to_y}, device_id_type=MESH,
+        )
+
+    def inject(step, j):
+        width = capacity
+        amp = wide(land.at[j], 0, rows_a_plane)
+        code = wide(land.at[j], rows_a_plane, rows_a_plane).astype(jnp.int32)
+        cell = code // kind_count
+        kind_hits = ones(rows_iota(kind_count, width) == code % kind_count)
+        picked = jnp.dot(table[step], kind_hits, preferred_element_type=F32)
+        currents = ((picked[:size] + picked[size:]) * amp).astype(BF16).astype(F32)
+        high = cell // low_count
+        left = jnp.concatenate(
+            [jnp.where(high == h, currents, 0.0).astype(BF16) for h in range(high_count)], axis=0
+        )
+        low_hits = ones(rows_iota(low_count, width) == cell % low_count)
+        inj[step] += lax.dot_general(left, low_hits, NT, preferred_element_type=F32)
+
+    def injected(step, c):
+        h, col = divmod(c * LANES, low_count)
+        return inj[step, h * size : (h + 1) * size, col : col + LANES]
+
+    together = 4
+
+    def inject_part(step, part, parts):
+        each = devices // parts
+
+        def body(q, carry):
+            for i in range(together):
+                inject(step, part * each + q * together + i)
+            return carry
+
+        lax.fori_loop(0, each // together, body, 0)
+
+    inputs = [
+        pltpu.make_async_copy(outside, inside, isem.at[i])
+        for i, (outside, inside) in enumerate((
+            (target_hbm, target), (v_hbm, v_in), (x_hbm, cond_x), (y_hbm, cond_y),
+            (cells_hbm, cells), (kinds_hbm, kinds), (amps_hbm, amps),
+            (waves_hbm, waves), (cap_hbm, cap), (via_hbm, via),
+        ))
+    ]
+    for copy in inputs:
+        copy.start()
     for e in range(halos):
-        for me, n, land in ((gx, nx, xl), (gy, ny, yl)):
+        for me, n, to in ((gx, nx, xl), (gy, ny, yl)):
             for side, last in ((0, 0), (1, n - 1)):
                 @pl.when(me == last)
                 def _():
-                    land[e, side] = jnp.zeros(land.shape[2:], F32)
+                    to[e, side] = jnp.zeros(to.shape[2:], F32)
+
+    @pl.when(gx == 0)
+    def _():
+        xc[...] = jnp.zeros_like(xc)
+
+    @pl.when(gy == 0)
+    def _():
+        yc[...] = jnp.zeros_like(yc)
 
     barrier = pltpu.get_barrier_semaphore()
-    for axis, me, n in (("gx", gx, nx), ("gy", gy, ny)):
-        for j in range(1, n):
-            pl.semaphore_signal(
-                barrier, inc=1, device_id={axis: lax.rem(me + j, n)}, device_id_type=MESH
-            )
-    pl.semaphore_wait(barrier, nx + ny - 2)
-
+
+    def greet(j, carry):
+        pl.semaphore_signal(
+            barrier, inc=1,
+            device_id={"gx": lax.rem(gx + j // ny, nx), "gy": lax.rem(gy + j % ny, ny)},
+            device_id_type=MESH,
+        )
+        return carry
+
+    lax.fori_loop(1, devices, greet, 0)
+    inputs[0].wait()
+    find_spots()
+    inputs[1].wait()
     rim = Rim()
     for c in range(count):
         f = v_in[pl.ds(c, size, stride=count), :]
-        v[c // tile_x, c % tile_x] = f
+        k1[c // tile_x, c % tile_x] = f
+        v[pl.ds(c, size, stride=count), :] = f
         rim.add(c, f)
-    start(x_copies(v, 0), gx, nx)
+    for copy in inputs[2:]:
+        copy.wait()
+    pl.semaphore_wait(barrier, devices - 1)
+    start(x_copies(k1, 0), gx, nx)
     rim.send(0)
-    arrive(v, 0)
+    rims = rim_copies()
+    pl.when(gx < nx - 1)(rims[0].start)
+    pl.when(gy < ny - 1)(rims[1].start)
+    fill_bins()
+
+    def start_bin(j, carry):
+        bin_copy(j).start()
+        return carry
+
+    lax.fori_loop(1, devices, start_bin, 0)
+    own = pl.multiple_of((gx * ny + gy) * SUBLANES, SUBLANES)
+    land[0] = send[pl.ds(own, SUBLANES), :]
+    wave_high, wave_low = halves(waves[...])
+    for step in range(steps):
+        at = slice(step * size, (step + 1) * size)
+        table[step, :size] = wave_high[at]
+        table[step, size:] = wave_low[at]
+    inj[...] = jnp.zeros_like(inj)
+    arrive(k1, 0)
+    for i, (me, n) in enumerate(((gx, nx), (gy, ny))):
+        pl.when(me > 0)(rims[i].wait_recv)
+        pl.when(me < n - 1)(rims[i].wait_send)
+    coefficients()
     rim = Rim()
 
     def first_residual(c, total):
         f = -SCALE * total
-        if c < tile_x:
-            f = f - inj[:size, c * LANES : (c + 1) * LANES]
         k0[c // tile_x, c % tile_x] = f
-        r[c // tile_x, c % tile_x] = f
+        if c >= tile_x:
+            rim.add(c, f)
+
+    stencil(k1, 0, 1, first_residual, lambda: None)
+
+    def first_inject(q, carry):
+        for i in range(together):
+            j = q * together + i
+            if i:
+                bin_copy(j).wait()
+            else:
+                pl.when(j > 0)(bin_copy(j).wait)
+        for i in range(together):
+            inject(0, q * together + i)
+        return carry
+
+    lax.fori_loop(0, devices // together, first_inject, 0)
+    for c in range(tile_x):
+        f = k0[0, c] - injected(0, c)
+        k0[0, c] = f
         rim.add(c, f)
-
-    stencil(v, 0, 1, first_residual, lambda: start(x_copies(k0, 1), gx, nx))
+    start(x_copies(k0, 1), gx, nx)
     rim.send(1)
 
     def time_step(step, carry):
         e = 1 + ITERS * step
+        more = step + 1 < steps
+
+        def inject_next(part):
+            @pl.when(more)
+            def _():
+                inject_part(step + 1, part, ITERS + 1)
+
         for c in range(count):
             split(0, c, k0[c // tile_x, c % tile_x])
         moments = grams([0], 0)
+        inject_next(0)
         for j in range(1, ITERS + 1):
             arrive(fields[j - 1], e + j - 1)
             if j > 1:
@@ -398,6 +526,7 @@
             moments = moments + grams([j - 1, j] if j < ITERS else [j - 1], j)
             add_start(step, j - 1, moments)
             moments = []
+            inject_next(j)
         m = add_finish(step, 0)
         add_turn(step, ITERS - 1)
         m = m + add_finish(step, 1)
@@ -427,7 +556,6 @@
         high, low = halves(both)
         turned = jnp.concatenate([high.astype(F32), low.astype(F32)], axis=1).T.astype(BF16)
         turned = jnp.concatenate([turned, turned], axis=1)
-        more = step + 1 < steps
         rim = Rim()
         pairs = sorted({c - c % 2 for c in edges})
         for n, c in enumerate(pairs + [c for c in range(0, count, 2) if c not in pairs]):
@@ -439,17 +567,14 @@
                 l, x = divmod(c + i, tile_x)
                 cols = slice(i * LANES, (i + 1) * LANES)
                 change = out[:size, cols]
-                v[l, x] = v[l, x] + change
+                rows = pl.ds(c + i, size, stride=count)
+                v[rows, :] = v[rows, :] + change
                 left = k0[l, x] + out[size:, cols]
-                r[l, x] = left
+                r[rows, :] = left
                 left = left + coef[8, c + i : c + i + 1, :] * change
                 if c + i < tile_x:
                     after = jnp.minimum(step + 1, steps - 1)
-                    here = slice((c + i) * LANES, (c + i + 1) * LANES)
-                    left = left - (
-                        inj[pl.ds(pl.multiple_of(after * size, size), size), here]
-                        - inj[pl.ds(pl.multiple_of(step * size, size), size), here]
-                    )
+                    left = left - (injected(after, c + i) - injected(step, c + i))
                 k0[l, x] = left
                 rim.add(c + i, left)
             if n + 1 == len(pairs):
@@ -466,71 +591,68 @@
     lax.fori_loop(0, steps, time_step, 0)
 
 
-def solve_grid(nx, ny, steps, layers, tile_x, volts, injected, coef):
-    size = injected.shape[0] // steps
+def body(volts, cap, cond_x, cond_y, via, waveforms, placement, cells, wave_ids, amps):
+    nx, ny = lax.axis_size("gx"), lax.axis_size("gy")
+    devices = nx * ny
+    size, layers, tile_x, tile_y = volts.shape
+    steps = waveforms.shape[0] // size
+    count = layers * tile_x
+    capacity = 2 * cells.shape[0] // devices
+    lane_count = min(capacity, 2 * LANES)
     halos = 1 + steps * ITERS
     packed = (2 * ITERS) * size * size // LANES
+    low_count = 2 * LANES
+    high_count = tile_x * tile_y // low_count
     field = (layers, tile_x, size, LANES)
     dma = pltpu.SemaphoreType.DMA
-    return pl.pallas_call(
-        functools.partial(grid_kernel, nx, ny, steps, layers, tile_x),
-        out_shape=[jax.ShapeDtypeStruct(field, F32)] * 2,
-        in_specs=[pl.BlockSpec(memory_space=pltpu.VMEM)] * 3,
+    flat = (count, tile_y)
+    many = (cells.shape[0] // LANES, LANES)
+    out, residual = pl.pallas_call(
+        functools.partial(grid_kernel, nx, ny, steps, layers, tile_x, capacity),
+        out_shape=[jax.ShapeDtypeStruct((size * count, LANES), F32)] * 2,
+        in_specs=[pl.BlockSpec(memory_space=pltpu.HBM)] * 10,
         out_specs=[pl.BlockSpec(memory_space=pltpu.VMEM)] * 2,
         scratch_shapes=[
+            pltpu.VMEM((size * count, LANES), F32),
+            *[pltpu.VMEM(flat, F32)] * 4,
+            pltpu.VMEM(waveforms.shape, F32),
+            *[pltpu.VMEM(many, jnp.int32)] * 3,
+            pltpu.VMEM(many, F32),
+            dma((10,)),
             pltpu.VMEM(field, F32),
             pltpu.VMEM(field, F32),
             pltpu.VMEM(field, F32),
-            pltpu.VMEM((2 * (ITERS + 1) * size, layers * tile_x * LANES), BF16),
+            pltpu.VMEM((2 * (ITERS + 1) * size, count * LANES), BF16),
             pltpu.VMEM((halos, 2, layers, size, LANES), F32),
             pltpu.VMEM((halos, 2, size, LANES), F32),
             pltpu.VMEM((halos, 2, size, LANES), F32),
             pltpu.VMEM((steps, nx, packed, LANES), F32),
             pltpu.VMEM((steps, ny, packed, LANES), F32),
+            pltpu.VMEM((9,) + flat, F32),
+            pltpu.VMEM(flat, F32),
+            pltpu.VMEM(flat, F32),
+            pltpu.VMEM(many, jnp.int32),
+            pltpu.VMEM((4 * devices * capacity // lane_count, lane_count), F32),
+            pltpu.VMEM((devices * SUBLANES, LANES), F32),
+            pltpu.VMEM((devices, SUBLANES, LANES), F32),
+            pltpu.VMEM((steps, 2 * size, waveforms.shape[1]), BF16),
+            pltpu.VMEM((steps, high_count * size, low_count), F32),
             dma((halos, 2)), dma((halos, 2)), dma((halos, 2)), dma((halos, 2)),
             dma((steps, ITERS, nx)), dma((steps, ITERS, nx)),
             dma((steps, ITERS, ny)), dma((steps, ITERS, ny)),
+            dma((2,)), dma((2,)), dma((devices,)), dma((devices,)),
         ],
         compiler_params=pltpu.CompilerParams(
-            collective_id=0, has_side_effects=True, vmem_limit_bytes=48 * 1024 * 1024
+            collective_id=0, has_side_effects=True, vmem_limit_bytes=67043328
         ),
-        name="grid",
-    )(volts, injected, coef)
-
-
-def shifted(x, axis):
-    length = lax.axis_size(axis)
-    return lax.ppermute(x, axis, [(i, i + 1) for i in range(length - 1)])
-
-
-def body(volts, cap, cond_x, cond_y, via, waveforms, placement, cells, wave_ids, amps):
-    nx, ny = lax.axis_size("gx"), lax.axis_size("gy")
-    devices = nx * ny
-    scenarios, layers, tile_x, tile_y = volts.shape
-    steps = waveforms.shape[0] // scenarios
-    capacity = 2 * cells.shape[0] // devices
-    slots = bin_instances(devices, capacity, placement[:, 0], cells, wave_ids, amps)
-    arrived = lax.all_to_all(
-        slots.reshape(2, devices, capacity), ("gx", "gy"), split_axis=1, concat_axis=1, tiled=True
+        name="transient",
+    )(
+        volts.reshape(-1, tile_y),
+        *[x.reshape(flat) for x in (cap, cond_x, cond_y, via)],
+        waveforms,
+        *[x.reshape(many) for x in (placement, cells, wave_ids, amps)],
     )
-    injected = inject(arrived, waveforms, tile_x * tile_y)
-    rim_x = shifted(cond_x[:, -1:, :], "gx")
-    rim_y = shifted(cond_y[:, :, -1:], "gy")
-    x_low = jnp.concatenate([rim_x, cond_x[:, :-1, :]], axis=1)
-    y_low = jnp.concatenate([rim_y, cond_y[:, :, :-1]], axis=2)
-    via_low = jnp.concatenate([jnp.zeros_like(via[:1]), via[:-1]], axis=0)
-    at_x = lax.broadcasted_iota(jnp.int32, cond_x.shape, 1) + lax.axis_index("gx") * tile_x
-    at_y = lax.broadcasted_iota(jnp.int32, cond_y.shape, 2) + lax.axis_index("gy") * tile_y
-    x_next = jnp.where(at_x == nx * tile_x - 1, 0.0, cond_x)
-    y_next = jnp.where(at_y == ny * tile_y - 1, 0.0, cond_y)
-    around = cond_x + x_low + cond_y + y_low + via + via_low
-    coef = jnp.stack([cap + around, around, x_next, x_low, y_next, y_low, via, via_low]) / SCALE
-    coef = jnp.concatenate([coef[:1] - SHIFT, coef[1:], cap[None]], axis=0)
-    coef = coef.reshape(9, layers * tile_x, tile_y)
-    out, residual = solve_grid(
-        nx, ny, steps, layers, tile_x, volts.reshape(-1, tile_y), injected, coef
-    )
-    return out.transpose(2, 0, 1, 3), residual.transpose(2, 0, 1, 3)
+    return out.reshape(volts.shape), residual.reshape(volts.shape)
 
 
 def solution(mesh):

time: 110 us -> 74.8 us (0.68)
  starting transfers between devices: 11.7 us -> 0 us
  local copies, waits for them, and re-layouts: 11.1 us -> 2.72 us
  waiting for transfers between devices: 7.28 us -> 0 us
  Pallas kernels: 76.9 us -> 71.2 us
    all_to_all x1 -> x0, waiting for transfers between devices: 7.28 us -> none  [body(): lax.all_to_all(slots.reshape(2, devices, capacity), ('gx', 'gy'), split_a...]
    ppermute x2 -> x0, starting transfers between devices: 6.67 us -> none  [shifted(): return lax.ppermute(x, axis, [(i, i + 1) for i in range(length - 1)])]
    pallas_call x3 -> x1, Pallas kernels: 76.9 us -> 71.2 us  [body(): pl.pallas_call(functools.partial(grid_kernel, nx, ny, steps, layers, tile...]
    all_to_all x1 -> x0, starting transfers between devices: 5.02 us -> none  [body(): lax.all_to_all(slots.reshape(2, devices, capacity), ('gx', 'gy'), split_a...]
    reshape x5 -> x0, local copies, waits for them, and re-layouts: 3.51 us -> none  [the longest x3 1.82 us: bin_instances(): x.reshape(shape)]
    unnamed x25 -> x4, local copies, waits for them, and re-layouts: 4.77 us -> 2.72 us
    slice x3 -> x0, local copies, waits for them, and re-layouts: 1.52 us -> none  [the longest x1 0.79 us: body(): rim_y = shifted(cond_y[:, :, -1:], 'gy')]
  transfers between devices with their start and end apart: 3 -> 0, of which waited for: 1 -> 0; matrix products, arithmetic and copies ran while one was open for 6% -> 0% of each run, Pallas kernels for 9% -> 0%
where the time goes in v2:
time: 74.8 us; the launch traced here: 74.6 us
  Pallas kernels  71.2 us (95%)
  local copies, waits for them, and re-layouts  2.72 us (4%)
    pallas_call x1, Pallas kernels, body(): pl.pallas_call(functools.partial(grid_kernel, nx, ny, steps, layers, tile...  71.2 us
    unnamed x4, local copies, waits for them, and re-layouts  2.72 us

profile of v2, /device:TPU:0, one launch (start us, length us, event | category | flops | bytes accessed | tf_op | source)
XLA Modules:
  0.0 74.6 jit_solution(1811885128665400413)
XLA Ops:
  0.6 71.2 %transient.1 = (f32[1024,128]{1,0:T(8,128)}, f32[1024,128]{1,0:T(8,128)}) custom-call(f32[1024,128]{1,0:T(8,128)} %bitcast.11, f32[32,128]{1,0:T(8,128)} %bitcast.18, f32[32,128]{1,0:T(8,128)} %bitcast.19, f32[32,128]{1,0:T(8,128)} %bitcast.20, f32[32,128]{1,0:T(8,128)} %bitcast.21, f32[64,64]{1,0:T(8,128)} %waves_hbm.1, s32[64,128]{1,0:T(8,128)} %bitcast.14, ...), custom_call_target="tpu_custom_call" | custom-call | tf_op jit(solution)/shard_map/transient/pallas_call | solution.py:610
  71.9 0.0 copy-start
  71.9 1.9 %copy.14 = f32[32,4,8,128]{3,2,1,0:T(8,128)} copy(f32[32,4,8,128]{3,2,1,0:T(8,128)} %bitcast.13) | data formatting | bytes 1048576
  73.8 0.0 copy-done
  73.8 0.8 %copy.15 = f32[32,4,8,128]{3,2,1,0:T(8,128)} copy(f32[32,4,8,128]{3,2,1,0:T(8,128)S(1)} %bitcast.12) | data formatting | bytes 1048576
Async XLA Ops:
  71.9 1.9 %copy-start = (f32[1024,128]{1,0:T(8,128)S(1)}, f32[1024,128]{1,0:T(8,128)}, u32[]{:S(2)}) copy-start(f32[1024,128]{1,0:T(8,128)} %get-tuple-element.5) | copy-start | bytes 1572868

commit v3 on v2

--- a/solution.py
+++ b/solution.py
@@ -24,6 +24,20 @@
 
 def ones(mask):
     return mask.astype(F32).astype(BF16)
+
+
+def picks(row, count):
+    lines = rows_iota(count, row.shape[1]).astype(F32).astype(BF16)
+    return jnp.where(lines == packed_row(row, count), BF16(1), BF16(0))
+
+
+def packed_row(row, count):
+    once = jnp.broadcast_to(row.astype(F32), (2 * SUBLANES, row.shape[1])).astype(BF16)
+    return jnp.concatenate([once] * (count // (2 * SUBLANES)), axis=0)
+
+
+def parted(x, count):
+    return x >> (count.bit_length() - 1), x & (count - 1)
 
 
 def wide(ref, row, count):
@@ -80,11 +94,11 @@
 def grid_kernel(
     nx, ny, steps, layers, tile_x, capacity,
     v_hbm, cap_hbm, x_hbm, y_hbm, via_hbm, waves_hbm, target_hbm, cells_hbm, kinds_hbm, amps_hbm,
-    v, r,
-    v_in, cap, cond_x, cond_y, via, waves, target, cells, kinds, amps, isem,
-    k0, k1, k2, basis, xl, ys, yl, gl, hl,
+    v_out, r_out,
+    v, r, cap, cond_x, cond_y, via, waves, target, cells, kinds, amps, isem, vsem, osem,
+    k0, k1, k2, k3, basis, xl, ys, yl, gl, hl, al,
     coef, xc, yc, spots, bins, send, land, table, inj,
-    xsend, xrecv, ysend, yrecv, gsend, grecv, hsend, hrecv, csend, crecv, asend, arecv,
+    xsend, xrecv, ysend, yrecv, gsend, grecv, hsend, hrecv, csend, crecv, asend, arecv, fsend, frecv,
 ):
     gx, gy = lax.axis_index("gx"), lax.axis_index("gy")
     size = xl.shape[3]
@@ -92,12 +106,12 @@
     halos = 1 + ITERS * steps
     packed = LANES // size
     part = size // packed
-    spans = ((0, 3 * part), (3 * part, 2 * part), (5 * part, part))
+    spans = ((0, 3 * part), (3 * part, 2 * part))
     lane = lax.broadcasted_iota(jnp.int32, (size, LANES), 1)
     group = lax.broadcasted_iota(jnp.int32, (part, LANES), 1) // size
     edges = [l * tile_x + x for l in range(layers) for x in (0, tile_x - 1)]
     inner = [c for c in range(count) if c not in edges]
-    fields = (k0, k1, k2)
+    fields = (k0, k1, k2, k3)
     devices = nx * ny
     low_count = inj.shape[2]
     high_count = inj.shape[1] // size
@@ -105,8 +119,14 @@
     lane_count = bins.shape[1]
     rows_a_plane = capacity // LANES
 
-    def at(ref, c):
-        return ref.at[c // tile_x, c % tile_x]
+    def xor(me, other, n):
+        for bit in range(n.bit_length() - 1):
+            power = 2**bit
+            me = me + power * ((other // power) % 2) * (1 - 2 * ((me // power) % 2))
+        return me
+
+    def peer(j):
+        return xor(gx, j % nx, nx), xor(gy, j // nx, ny)
 
     def x_copies(src, e):
         return [
@@ -122,7 +142,7 @@
     def y_copies(e):
         return [
             pltpu.make_async_remote_copy(
-                ys.at[e, side], yl.at[e, side], ysend.at[e, side], yrecv.at[e, side],
+                ys.at[e], yl.at[e, side], ysend.at[e, side], yrecv.at[e, side],
                 device_id={"gy": lax.rem(gy + (1 if side == 0 else ny - 1), ny)},
                 device_id_type=MESH,
             )
@@ -150,41 +170,44 @@
 
     class Rim:
         def __init__(self):
-            self.last = jnp.zeros((size, LANES), F32)
-            self.first = self.last
+            self.both = jnp.zeros((size, LANES), F32)
 
         def add(self, c, f):
-            self.last = jnp.where(lane == c, pltpu.roll(f, (c + 1) % LANES, 1), self.last)
-            self.first = jnp.where(lane == c, pltpu.roll(f, c, 1) if c else f, self.first)
+            self.both = jnp.where(lane // 2 == c, pltpu.roll(f, 2 * c + 1, 1), self.both)
 
         def send(self, e):
-            ys[e, 0] = self.last
-            ys[e, 1] = self.first
+            ys[e] = self.both
             start(y_copies(e), gy, ny)
 
-    def stencil(src, e, own, emit, after_edges):
-        y_low, y_high = yl[e, 0], yl[e, 1]
+    def k(i, c):
+        return coef[i, c : c + 1, :]
+
+    def inside(src, own, dst):
+        for c in range(count):
+            l, x = divmod(c, tile_x)
+            f = src[l, x]
+            total = k(own, c) * f
+            if x + 1 < tile_x:
+                total = total - k(2, c) * src[l, x + 1]
+            if x:
+                total = total - k(3, c) * src[l, x - 1]
+            total = total - k(4, c) * pltpu.roll(f, LANES - 1, 1) - k(5, c) * pltpu.roll(f, 1, 1)
+            if l + 1 < layers:
+                total = total - k(6, c) * src[l + 1, x]
+            if l:
+                total = total - k(7, c) * src[l - 1, x]
+            dst[l, x] = total
+
+    def outside(dst, e, emit, after_edges):
+        rims = jnp.where(lane % 2 == 0, yl[e, 0], pltpu.roll(yl[e, 1], LANES - 2, 1))
         for n, c in enumerate(edges + inner):
             l, x = divmod(c, tile_x)
-            f = src[l, x]
-
-            def k(i):
-                return coef[i, c : c + 1, :]
-
-            high = src[l, x + 1] if x + 1 < tile_x else xl[e, 1, l]
-            low = src[l, x - 1] if x else xl[e, 0, l]
-            total = k(own) * f - k(2) * high - k(3) * low
-            after = jnp.where(
-                lane == LANES - 1, pltpu.roll(y_high, LANES - 1 - c, 1), pltpu.roll(f, LANES - 1, 1)
-            )
-            ahead = jnp.where(
-                lane == 0, pltpu.roll(y_low, LANES - c, 1) if c else y_low, pltpu.roll(f, 1, 1)
-            )
-            total = total - k(4) * after - k(5) * ahead
-            if l + 1 < layers:
-                total = total - k(6) * src[l + 1, x]
-            if l:
-                total = total - k(7) * src[l - 1, x]
+            moved = pltpu.roll(rims, LANES - 2 * c, 1) if c else rims
+            total = dst[l, x] - k(8, c) * moved
+            if x + 1 == tile_x:
+                total = total - k(2, c) * xl[e, 1, l]
+            if x == 0:
+                total = total - k(3, c) * xl[e, 0, l]
             emit(c, total)
             if n + 1 == len(edges):
                 after_edges()
@@ -254,6 +277,34 @@
     def add_finish(step, g):
         total = landed(hl, along_y(step, g), step, g, ny)
         return [total[i * part : (i + 1) * part] for i in range(spans[g][1] // part)]
+
+    def every_copy(step, j):
+        to_x, to_y = peer(j)
+        me = gx * ny + gy
+        return pltpu.make_async_remote_copy(
+            al.at[step, me], al.at[step, me], fsend.at[step, j], frecv.at[step, j],
+            device_id={"gx": to_x, "gy": to_y}, device_id_type=MESH,
+        )
+
+    def every_start(step, matrix):
+        al[step, gx * ny + gy] = pack(matrix)
+
+        def body(i, carry):
+            every_copy(step, devices - 1 - i).start()
+            return carry
+
+        lax.fori_loop(0, devices - 1, body, 0)
+
+    def every_finish(step):
+        def body(j, carry):
+            every_copy(step, j).wait()
+            return carry
+
+        lax.fori_loop(1, devices, body, 0)
+        terms = [al[step, j] for j in range(devices)]
+        while len(terms) > 1:
+            terms = [a + b for a, b in zip(terms[::2], terms[1::2])]
+        return terms[0]
 
     def place(matrix, g, block):
         shift = ((block - g) * size) % LANES
@@ -281,11 +332,14 @@
             x_end = jnp.logical_and(row == tile_x - 1, gx == nx - 1)
             y_end = jnp.logical_and(col == LANES - 1, gy == ny - 1)
             around = cond_x[at] + x_low + cond_y[at] + y_low + via[at] + above
+            first, final = col == 0, col == LANES - 1
+            y_next = jnp.where(y_end, 0.0, cond_y[at])
             values = [
                 (cap[at] + around) / SCALE - SHIFT, around / SCALE,
                 jnp.where(x_end, 0.0, cond_x[at]) / SCALE, x_low / SCALE,
-                jnp.where(y_end, 0.0, cond_y[at]) / SCALE, y_low / SCALE,
-                via[at] / SCALE, above / SCALE, cap[at],
+                jnp.where(final, 0.0, y_next) / SCALE, jnp.where(first, 0.0, y_low) / SCALE,
+                via[at] / SCALE, above / SCALE,
+                jnp.where(final, y_next, jnp.where(first, y_low, 0.0)) / SCALE, cap[at],
             ]
             for i, value in enumerate(values):
                 coef[i, at] = value
@@ -294,7 +348,7 @@
     def find_spots():
         width = 2 * LANES
         before = ones(rows_iota(width, width) < lax.broadcasted_iota(jnp.int32, (width, width), 1))
-        together = 4
+        together = 8
 
         def body(q, base):
             hits = [
@@ -320,22 +374,27 @@
     def fill_bins():
         rows = bins.shape[0] // 4
         width = 4 * LANES
+        each = 2
         bins[...] = jnp.zeros_like(bins)
 
-        def body(b, carry):
-            spot = wide(spots, b * 4, 4)
-            key = wide(target, b * 4, 4) + (spot // lane_count) * devices
-            mask = rows_iota(rows, width) == key
-            there = ones(rows_iota(lane_count, width) == spot % lane_count)
+        def one(b):
+            upper, lower = parted(wide(spots, b * 4, 4), lane_count)
+            key = wide(target, b * 4, 4) + upper * devices
+            hits = rows_iota(rows, width).astype(F32).astype(BF16) == packed_row(key, rows)
             code = wide(cells, b * 4, 4) * kind_count + wide(kinds, b * 4, 4)
             amp = wide(amps, b * 4, 4)
             amp_high = amp.astype(BF16).astype(F32)
-            parts = (amp_high, amp - amp_high, (code >> 8).astype(F32), (code & 255).astype(F32))
-            left = jnp.concatenate([jnp.where(mask, p, 0.0).astype(BF16) for p in parts], axis=0)
+            parts = (amp_high, amp - amp_high, code >> 8, code & 255)
+            left = [jnp.where(hits, packed_row(p, rows), BF16(0)) for p in parts]
+            return jnp.concatenate(left, axis=0), picks(lower, lane_count)
+
+        def body(b, carry):
+            pairs = [one(b * each + i) for i in range(each)]
+            left, there = (jnp.concatenate(x, axis=1) for x in zip(*pairs))
             bins[...] += lax.dot_general(left, there, NT, preferred_element_type=F32)
             return carry
 
-        lax.fori_loop(0, target.shape[0] // 4, body, 0, unroll=2)
+        lax.fori_loop(0, target.shape[0] // (4 * each), body, 0, unroll=2)
         planes = (
             bins[:rows] + bins[rows : 2 * rows],
             bins[2 * rows : 3 * rows] * 256.0 + bins[3 * rows :],
@@ -350,28 +409,27 @@
                 ]
 
     def bin_copy(j):
-        to_x = lax.rem(gx + j // ny, nx)
-        to_y = lax.rem(gy + j % ny, ny)
+        to_x, to_y = peer(j)
         at = pl.multiple_of((to_x * ny + to_y) * SUBLANES, SUBLANES)
         return pltpu.make_async_remote_copy(
             send.at[pl.ds(at, SUBLANES)], land.at[j], asend.at[j], arecv.at[j],
             device_id={"gx": to_x, "gy": to_y}, device_id_type=MESH,
         )
 
-    def inject(step, j):
-        width = capacity
-        amp = wide(land.at[j], 0, rows_a_plane)
-        code = wide(land.at[j], rows_a_plane, rows_a_plane).astype(jnp.int32)
-        cell = code // kind_count
-        kind_hits = ones(rows_iota(kind_count, width) == code % kind_count)
-        picked = jnp.dot(table[step], kind_hits, preferred_element_type=F32)
-        currents = ((picked[:size] + picked[size:]) * amp).astype(BF16).astype(F32)
-        high = cell // low_count
-        left = jnp.concatenate(
-            [jnp.where(high == h, currents, 0.0).astype(BF16) for h in range(high_count)], axis=0
-        )
-        low_hits = ones(rows_iota(low_count, width) == cell % low_count)
-        inj[step] += lax.dot_general(left, low_hits, NT, preferred_element_type=F32)
+    def inject(step, sources):
+        def one(j):
+            amp = wide(land.at[j], 0, rows_a_plane)
+            code = wide(land.at[j], rows_a_plane, rows_a_plane).astype(jnp.int32)
+            cell, kind = parted(code, kind_count)
+            upper, lower = parted(cell, low_count)
+            picked = jnp.dot(table[step], picks(kind, kind_count), preferred_element_type=F32)
+            currents = ((picked[:size] + picked[size:]) * amp).astype(BF16)
+            high = packed_row(upper, size)
+            left = [jnp.where(high == BF16(h), currents, BF16(0)) for h in range(high_count)]
+            return jnp.concatenate(left, axis=0), picks(lower, low_count)
+
+        left, hits = (jnp.concatenate(x, axis=1) for x in zip(*[one(j) for j in sources]))
+        inj[step] += lax.dot_general(left, hits, NT, preferred_element_type=F32)
 
     def injected(step, c):
         h, col = divmod(c * LANES, low_count)
@@ -383,21 +441,23 @@
         each = devices // parts
 
         def body(q, carry):
-            for i in range(together):
-                inject(step, part * each + q * together + i)
+            inject(step, [part * each + q * together + i for i in range(together)])
             return carry
 
         lax.fori_loop(0, each // together, body, 0)
 
     inputs = [
-        pltpu.make_async_copy(outside, inside, isem.at[i])
-        for i, (outside, inside) in enumerate((
-            (target_hbm, target), (v_hbm, v_in), (x_hbm, cond_x), (y_hbm, cond_y),
-            (cells_hbm, cells), (kinds_hbm, kinds), (amps_hbm, amps),
-            (waves_hbm, waves), (cap_hbm, cap), (via_hbm, via),
+        pltpu.make_async_copy(there, here, isem.at[i])
+        for i, (there, here) in enumerate((
+            (target_hbm, target), (cells_hbm, cells), (kinds_hbm, kinds), (amps_hbm, amps),
+            (x_hbm, cond_x), (y_hbm, cond_y), (cap_hbm, cap), (via_hbm, via), (waves_hbm, waves),
         ))
     ]
-    for copy in inputs:
+    fetches = [
+        pltpu.make_async_copy(v_hbm.at[:, c], v.at[c // tile_x, c % tile_x], vsem.at[c])
+        for c in range(count)
+    ]
+    for copy in inputs[:4] + fetches + inputs[4:]:
         copy.start()
     for e in range(halos):
         for me, n, to in ((gx, nx, xl), (gy, ny, yl)):
@@ -427,28 +487,27 @@
     lax.fori_loop(1, devices, greet, 0)
     inputs[0].wait()
     find_spots()
-    inputs[1].wait()
+    for copy in inputs[1:4]:
+        copy.wait()
+    fill_bins()
+    for copy in fetches + inputs[4:]:
+        copy.wait()
     rim = Rim()
     for c in range(count):
-        f = v_in[pl.ds(c, size, stride=count), :]
-        k1[c // tile_x, c % tile_x] = f
-        v[pl.ds(c, size, stride=count), :] = f
-        rim.add(c, f)
-    for copy in inputs[2:]:
-        copy.wait()
+        rim.add(c, v[c // tile_x, c % tile_x])
     pl.semaphore_wait(barrier, devices - 1)
-    start(x_copies(k1, 0), gx, nx)
-    rim.send(0)
+
     rims = rim_copies()
     pl.when(gx < nx - 1)(rims[0].start)
     pl.when(gy < ny - 1)(rims[1].start)
-    fill_bins()
-
-    def start_bin(j, carry):
-        bin_copy(j).start()
+
+    def start_bin(i, carry):
+        bin_copy(devices - 1 - i).start()
         return carry
 
-    lax.fori_loop(1, devices, start_bin, 0)
+    lax.fori_loop(0, devices - 1, start_bin, 0)
+    start(x_copies(v, 0), gx, nx)
+    rim.send(0)
     own = pl.multiple_of((gx * ny + gy) * SUBLANES, SUBLANES)
     land[0] = send[pl.ds(own, SUBLANES), :]
     wave_high, wave_low = halves(waves[...])
@@ -457,20 +516,6 @@
         table[step, :size] = wave_high[at]
         table[step, size:] = wave_low[at]
     inj[...] = jnp.zeros_like(inj)
-    arrive(k1, 0)
-    for i, (me, n) in enumerate(((gx, nx), (gy, ny))):
-        pl.when(me > 0)(rims[i].wait_recv)
-        pl.when(me < n - 1)(rims[i].wait_send)
-    coefficients()
-    rim = Rim()
-
-    def first_residual(c, total):
-        f = -SCALE * total
-        k0[c // tile_x, c % tile_x] = f
-        if c >= tile_x:
-            rim.add(c, f)
-
-    stencil(k1, 0, 1, first_residual, lambda: None)
 
     def first_inject(q, carry):
         for i in range(together):
@@ -479,14 +524,32 @@
                 bin_copy(j).wait()
             else:
                 pl.when(j > 0)(bin_copy(j).wait)
-        for i in range(together):
-            inject(0, q * together + i)
+        inject(0, [q * together + i for i in range(together)])
         return carry
 
-    lax.fori_loop(0, devices // together, first_inject, 0)
+    for i, (me, n) in enumerate(((gx, nx), (gy, ny))):
+        pl.when(me > 0)(rims[i].wait_recv)
+        pl.when(me < n - 1)(rims[i].wait_send)
+    coefficients()
+    inside(v, 1, k0)
+    early = nx // together
+    lax.fori_loop(0, early, first_inject, 0)
+    arrive(v, 0)
+    rim = Rim()
+
+    def first_residual(c, total):
+        f = -SCALE * total
+        k0[c // tile_x, c % tile_x] = f
+        if c >= tile_x:
+            split(0, c, f)
+            rim.add(c, f)
+
+    outside(k0, 0, first_residual, lambda: None)
+    lax.fori_loop(early, devices // together, first_inject, 0)
     for c in range(tile_x):
         f = k0[0, c] - injected(0, c)
         k0[0, c] = f
+        split(0, c, f)
         rim.add(c, f)
     start(x_copies(k0, 1), gx, nx)
     rim.send(1)
@@ -500,9 +563,8 @@
             def _():
                 inject_part(step + 1, part, ITERS + 1)
 
-        for c in range(count):
-            split(0, c, k0[c // tile_x, c % tile_x])
         moments = grams([0], 0)
+        inside(k0, 0, k1)
         inject_next(0)
         for j in range(1, ITERS + 1):
             arrive(fields[j - 1], e + j - 1)
@@ -520,16 +582,17 @@
                 if j < ITERS:
                     start(x_copies(fields[j], e + j), gx, nx)
 
-            stencil(fields[j - 1], e + j - 1, 0, next_field, send_edges)
+            outside(fields[j], e + j - 1, next_field, send_edges)
             if j < ITERS:
                 rim.send(e + j)
-            moments = moments + grams([j - 1, j] if j < ITERS else [j - 1], j)
-            add_start(step, j - 1, moments)
-            moments = []
+                moments = moments + grams([j - 1, j], j)
+                inside(fields[j], 0, fields[j + 1])
+                add_start(step, j - 1, moments)
+                moments = []
+            else:
+                every_start(step, grams([j - 1], j)[0])
             inject_next(j)
-        m = add_finish(step, 0)
-        add_turn(step, ITERS - 1)
-        m = m + add_finish(step, 1)
+        m = add_finish(step, 0) + add_finish(step, 1)
         m.append(jnp.zeros_like(m[0]))
         shifted_m = [SCALE * (m[i + 1] + SHIFT * m[i]) for i in range(len(m) - 1)]
         tiles = []
@@ -542,9 +605,9 @@
         early = (ITERS - 1) * packed
         for p in range(early):
             tiles = eliminate_panel(tiles, p)
-        (final,) = add_finish(step, ITERS - 1)
+        last = every_finish(step)
         for g in range(packed):
-            at_end = jnp.where(group == ITERS - 1, SCALE * place(final, g, ITERS - 1), 0.0)
+            at_end = jnp.where(group == ITERS - 1, SCALE * place(last, g, ITERS - 1), 0.0)
             tiles[early + g] = tiles[early + g] + at_end
         for p in range(early, ITERS * packed):
             tiles = eliminate_panel(tiles, p)
@@ -567,15 +630,15 @@
                 l, x = divmod(c + i, tile_x)
                 cols = slice(i * LANES, (i + 1) * LANES)
                 change = out[:size, cols]
-                rows = pl.ds(c + i, size, stride=count)
-                v[rows, :] = v[rows, :] + change
+                v[l, x] = v[l, x] + change
                 left = k0[l, x] + out[size:, cols]
-                r[rows, :] = left
-                left = left + coef[8, c + i : c + i + 1, :] * change
+                r[l, x] = left
+                left = left + k(9, c + i) * change
                 if c + i < tile_x:
                     after = jnp.minimum(step + 1, steps - 1)
                     left = left - (injected(after, c + i) - injected(step, c + i))
                 k0[l, x] = left
+                split(0, c + i, left)
                 rim.add(c + i, left)
             if n + 1 == len(pairs):
                 @pl.when(more)
@@ -589,6 +652,57 @@
         return carry
 
     lax.fori_loop(0, steps, time_step, 0)
+    stores = []
+    for i, (here, there) in enumerate(((v, v_out), (r, r_out))):
+        for c in range(count):
+            stores.append(
+                pltpu.make_async_copy(here.at[c // tile_x, c % tile_x], there.at[:, c], osem.at[i, c])
+            )
+            stores[-1].start()
+    for copy in stores:
+        copy.wait()
+
+
+def hand_over_kernel(first, second, first_out, second_out, held, fetched, stored):
+    pairs = ((first, first_out), (second, second_out))
+    chunks = held.shape[1]
+    each = first.shape[0] // chunks
+
+    def fetch(i, n):
+        return pltpu.make_async_copy(
+            pairs[i][0].at[pl.ds(n * each, each)], held.at[i, n], fetched.at[i, n]
+        )
+
+    def store(i, n):
+        return pltpu.make_async_copy(
+            held.at[i, n], pairs[i][1].at[pl.ds(n * each, each)], stored.at[i, n]
+        )
+
+    order = [(i, n) for n in range(chunks) for i in range(2)]
+    for where in order:
+        fetch(*where).start()
+    for where in order:
+        fetch(*where).wait()
+        store(*where).start()
+    for where in order:
+        store(*where).wait()
+
+
+def hand_over(first, second):
+    chunks = 4
+    dma = pltpu.SemaphoreType.DMA
+    return pl.pallas_call(
+        hand_over_kernel,
+        out_shape=[jax.ShapeDtypeStruct(first.shape, F32)] * 2,
+        in_specs=[pl.BlockSpec(memory_space=pltpu.HBM)] * 2,
+        out_specs=[pl.BlockSpec(memory_space=pltpu.HBM)] * 2,
+        scratch_shapes=[
+            pltpu.VMEM((2, chunks, first.shape[0] // chunks) + first.shape[1:], F32),
+            dma((2, chunks)), dma((2, chunks)),
+        ],
+        compiler_params=pltpu.CompilerParams(vmem_limit_bytes=67043328),
+        name="hand_over",
+    )(first, second)
 
 
 def body(volts, cap, cond_x, cond_y, via, waveforms, placement, cells, wave_ids, amps):
@@ -600,7 +714,7 @@
     capacity = 2 * cells.shape[0] // devices
     lane_count = min(capacity, 2 * LANES)
     halos = 1 + steps * ITERS
-    packed = (2 * ITERS) * size * size // LANES
+    packed = (2 * ITERS - 1) * size * size // LANES
     low_count = 2 * LANES
     high_count = tile_x * tile_y // low_count
     field = (layers, tile_x, size, LANES)
@@ -609,26 +723,29 @@
     many = (cells.shape[0] // LANES, LANES)
     out, residual = pl.pallas_call(
         functools.partial(grid_kernel, nx, ny, steps, layers, tile_x, capacity),
-        out_shape=[jax.ShapeDtypeStruct((size * count, LANES), F32)] * 2,
+        out_shape=[jax.ShapeDtypeStruct((size, count, LANES), F32)] * 2,
         in_specs=[pl.BlockSpec(memory_space=pltpu.HBM)] * 10,
-        out_specs=[pl.BlockSpec(memory_space=pltpu.VMEM)] * 2,
+        out_specs=[pl.BlockSpec(memory_space=pltpu.HBM)] * 2,
         scratch_shapes=[
-            pltpu.VMEM((size * count, LANES), F32),
+            pltpu.VMEM(field, F32),
+            pltpu.VMEM(field, F32),
             *[pltpu.VMEM(flat, F32)] * 4,
             pltpu.VMEM(waveforms.shape, F32),
             *[pltpu.VMEM(many, jnp.int32)] * 3,
             pltpu.VMEM(many, F32),
-            dma((10,)),
+            dma((9,)), dma((count,)), dma((2, count)),
+            pltpu.VMEM(field, F32),
             pltpu.VMEM(field, F32),
             pltpu.VMEM(field, F32),
             pltpu.VMEM(field, F32),
             pltpu.VMEM((2 * (ITERS + 1) * size, count * LANES), BF16),
             pltpu.VMEM((halos, 2, layers, size, LANES), F32),
-            pltpu.VMEM((halos, 2, size, LANES), F32),
+            pltpu.VMEM((halos, size, LANES), F32),
             pltpu.VMEM((halos, 2, size, LANES), F32),
             pltpu.VMEM((steps, nx, packed, LANES), F32),
             pltpu.VMEM((steps, ny, packed, LANES), F32),
-            pltpu.VMEM((9,) + flat, F32),
+            pltpu.VMEM((steps, devices, size * size // LANES, LANES), F32),
+            pltpu.VMEM((10,) + flat, F32),
             pltpu.VMEM(flat, F32),
             pltpu.VMEM(flat, F32),
             pltpu.VMEM(many, jnp.int32),
@@ -641,17 +758,19 @@
             dma((steps, ITERS, nx)), dma((steps, ITERS, nx)),
             dma((steps, ITERS, ny)), dma((steps, ITERS, ny)),
             dma((2,)), dma((2,)), dma((devices,)), dma((devices,)),
+            dma((steps, devices)), dma((steps, devices)),
         ],
         compiler_params=pltpu.CompilerParams(
             collective_id=0, has_side_effects=True, vmem_limit_bytes=67043328
         ),
         name="transient",
     )(
-        volts.reshape(-1, tile_y),
+        volts.reshape(size, count, tile_y),
         *[x.reshape(flat) for x in (cap, cond_x, cond_y, via)],
         waveforms,
         *[x.reshape(many) for x in (placement, cells, wave_ids, amps)],
     )
+    out, residual = hand_over(out, residual)
     return out.reshape(volts.shape), residual.reshape(volts.shape)
 
 

time: 74.8 us -> 68.9 us (0.921)
  Pallas kernels: 71.2 us -> 68.1 us
  local copies, waits for them, and re-layouts: 2.72 us -> 0 us
    pallas_call x1, Pallas kernels: 71.2 us -> 66 us  [body(): pl.pallas_call(functools.partial(grid_kernel, nx, ny, steps, layers, tile...]
    unnamed x4 -> x0, local copies, waits for them, and re-layouts: 2.72 us -> none
    pallas_call x0 -> x1, Pallas kernels: none -> 2.09 us  [hand_over(): pl.pallas_call(hand_over_kernel, out_shape=[jax.ShapeDtypeStruct(first.sh...]
where the time goes in v3:
time: 68.9 us; the launch traced here: 68.7 us
  Pallas kernels  68.1 us (99%)
    pallas_call x1, Pallas kernels, body(): pl.pallas_call(functools.partial(grid_kernel, nx, ny, steps, layers, tile...  66 us
    pallas_call x1, Pallas kernels, hand_over(): pl.pallas_call(hand_over_kernel, out_shape=[jax.ShapeDtypeStruct(first.sh...  2.09 us

profile of v3, /device:TPU:0, one launch (start us, length us, event | category | flops | bytes accessed | tf_op | source)
XLA Modules:
  0.0 68.7 jit_solution(13531816891570541998)
XLA Ops:
  0.6 66.0 %transient.1 = (f32[32,32,128]{2,1,0:T(8,128)}, f32[32,32,128]{2,1,0:T(8,128)}) custom-call(f32[32,32,128]{2,1,0:T(8,128)} %bitcast.11, f32[32,128]{1,0:T(8,128)} %bitcast.16, f32[32,128]{1,0:T(8,128)} %bitcast.17, f32[32,128]{1,0:T(8,128)} %bitcast.18, f32[32,128]{1,0:T(8,128)} %bitcast.19, f32[64,64]{1,0:T(8,128)} %waves_hbm.1, s32[64,128]{1,0:T(8,128)} %bitcast.12, ...), custom_call_target="tpu_custom_call" | custom-call | tf_op jit(solution)/shard_map/transient/pallas_call | solution.py:724
  66.6 2.1 %hand_over.1 = (f32[32,32,128]{2,1,0:T(8,128)}, f32[32,32,128]{2,1,0:T(8,128)}) custom-call(f32[32,32,128]{2,1,0:T(8,128)} %get-tuple-element.6.first, f32[32,32,128]{2,1,0:T(8,128)} %get-tuple-element.7.second), custom_call_target="tpu_custom_call" | custom-call | tf_op jit(solution)/shard_map/hand_over/pallas_call | solution.py:694

commit v4 on v3

--- a/solution.py
+++ b/solution.py
@@ -91,17 +91,21 @@
     return high, (x - high.astype(F32)).astype(BF16)
 
 
+def settle(ref, semaphore):
+    pltpu.make_async_copy(ref, ref, semaphore).wait()
+
+
 def grid_kernel(
     nx, ny, steps, layers, tile_x, capacity,
     v_hbm, cap_hbm, x_hbm, y_hbm, via_hbm, waves_hbm, target_hbm, cells_hbm, kinds_hbm, amps_hbm,
     v_out, r_out,
     v, r, cap, cond_x, cond_y, via, waves, target, cells, kinds, amps, isem, vsem, osem,
-    k0, k1, k2, k3, basis, xl, ys, yl, gl, hl, al,
+    k0, k1, k2, k3, basis, xs, xl, ys, yl, gl, hl, al,
     coef, xc, yc, spots, bins, send, land, table, inj,
     xsend, xrecv, ysend, yrecv, gsend, grecv, hsend, hrecv, csend, crecv, asend, arecv, fsend, frecv,
 ):
     gx, gy = lax.axis_index("gx"), lax.axis_index("gy")
-    size = xl.shape[3]
+    size = xs.shape[3]
     count = layers * tile_x
     halos = 1 + ITERS * steps
     packed = LANES // size
@@ -118,23 +122,25 @@
     kind_count = waves.shape[1]
     lane_count = bins.shape[1]
     rows_a_plane = capacity // LANES
-
-    def xor(me, other, n):
-        for bit in range(n.bit_length() - 1):
-            power = 2**bit
-            me = me + power * ((other // power) % 2) * (1 - 2 * ((me // power) % 2))
-        return me
+    together = 4
+
+    def walk(me, n):
+        flips = [2**b * (1 - 2 * ((me // 2**b) % 2)) for b in range(n.bit_length() - 1)]
+        places = [me]
+        for flip in flips:
+            places += [place + flip for place in places]
+        return places
+
+    walk_x, walk_y = walk(gx, nx), walk(gy, ny)
 
     def peer(j):
-        return xor(gx, j % nx, nx), xor(gy, j // nx, ny)
-
-    def x_copies(src, e):
+        return walk_x[j % nx], walk_y[j // nx]
+
+    def x_copies(e):
         return [
             pltpu.make_async_remote_copy(
-                src.at[:, tile_x - 1 if side == 0 else 0], xl.at[e, side],
-                xsend.at[e, side], xrecv.at[e, side],
-                device_id={"gx": lax.rem(gx + (1 if side == 0 else nx - 1), nx)},
-                device_id_type=MESH,
+                xs.at[e, side], xl.at[e, side], xsend.at[e % 2, side], xrecv.at[e % 2, side],
+                device_id={"gx": gx + (1 if side == 0 else -1)}, device_id_type=MESH,
             )
             for side in range(2)
         ]
@@ -142,8 +148,8 @@
     def y_copies(e):
         return [
             pltpu.make_async_remote_copy(
-                ys.at[e], yl.at[e, side], ysend.at[e, side], yrecv.at[e, side],
-                device_id={"gy": lax.rem(gy + (1 if side == 0 else ny - 1), ny)},
+                ys.at[e], yl.at[e, side], ysend.at[e % 2, side], yrecv.at[e % 2, side],
+                device_id={"gy": gy + (1 if side == 0 else -1)},
                 device_id_type=MESH,
             )
             for side in range(2)
@@ -164,20 +170,28 @@
             copies[1].wait_recv()
             copies[0].wait_send()
 
-    def arrive(src, e):
-        finish(x_copies(src, e), gx, nx)
+    def arrive(e):
+        finish(x_copies(e), gx, nx)
         finish(y_copies(e), gy, ny)
 
     class Rim:
-        def __init__(self):
+        def __init__(self, e):
+            self.e = e
             self.both = jnp.zeros((size, LANES), F32)
 
         def add(self, c, f):
+            l, x = divmod(c, tile_x)
+            for side, edge in ((0, tile_x - 1), (1, 0)):
+                if x == edge:
+                    xs[self.e, side, l] = f.astype(BF16)
             self.both = jnp.where(lane // 2 == c, pltpu.roll(f, 2 * c + 1, 1), self.both)
 
-        def send(self, e):
-            ys[e] = self.both
-            start(y_copies(e), gy, ny)
+        def send_x(self):
+            start(x_copies(self.e), gx, nx)
+
+        def send_y(self):
+            ys[self.e] = self.both
+            start(y_copies(self.e), gy, ny)
 
     def k(i, c):
         return coef[i, c : c + 1, :]
@@ -205,9 +219,9 @@
             moved = pltpu.roll(rims, LANES - 2 * c, 1) if c else rims
             total = dst[l, x] - k(8, c) * moved
             if x + 1 == tile_x:
-                total = total - k(2, c) * xl[e, 1, l]
+                total = total - k(2, c) * xl[e, 1, l].astype(F32)
             if x == 0:
-                total = total - k(3, c) * xl[e, 0, l]
+                total = total - k(3, c) * xl[e, 0, l].astype(F32)
             emit(c, total)
             if n + 1 == len(edges):
                 after_edges()
@@ -236,22 +250,22 @@
     def pack(matrix):
         return jnp.concatenate([matrix[i * part : (i + 1) * part] for i in range(packed)], axis=1)
 
-    def gather(land, step, g, ssem, rsem, axis, me, n):
+    def gather(land, step, g, ssem, rsem, axis, places):
         rows = pl.ds(spans[g][0], spans[g][1])
         return [
             pltpu.make_async_remote_copy(
-                land.at[step, me, rows], land.at[step, me, rows],
-                ssem.at[step, g, j], rsem.at[step, g, j],
-                device_id={axis: lax.rem(me + j, n)}, device_id_type=MESH,
+                land.at[step, places[0], rows], land.at[step, places[0], rows],
+                ssem.at[step, g], rsem.at[step, g],
+                device_id={axis: places[j]}, device_id_type=MESH,
             )
-            for j in range(1, n)
+            for j in range(1, len(places))
         ]
 
     def along_x(step, g):
-        return gather(gl, step, g, gsend, grecv, "gx", gx, nx)
+        return gather(gl, step, g, gsend, grecv, "gx", walk_x)
 
     def along_y(step, g):
-        return gather(hl, step, g, hsend, hrecv, "gy", gy, ny)
+        return gather(hl, step, g, hsend, hrecv, "gy", walk_y)
 
     def add_start(step, g, matrices):
         for i, matrix in enumerate(matrices):
@@ -259,48 +273,41 @@
         for copy in along_x(step, g):
             copy.start()
 
-    def landed(land, copies, step, g, n):
-        for copy in copies:
-            copy.wait()
+    def landed(land, ssem, rsem, step, g, n):
         first, rows = spans[g]
+        for semaphore in (ssem, rsem):
+            settle(land.at[step, pl.ds(0, n - 1), pl.ds(first, rows)], semaphore.at[step, g])
         total = land[step, 0, first : first + rows, :]
         for j in range(1, n):
             total = total + land[step, j, first : first + rows, :]
         return total
 
     def add_turn(step, g):
-        total = landed(gl, along_x(step, g), step, g, nx)
+        total = landed(gl, gsend, grecv, step, g, nx)
         hl[step, gy, pl.ds(*spans[g]), :] = total
         for copy in along_y(step, g):
             copy.start()
 
     def add_finish(step, g):
-        total = landed(hl, along_y(step, g), step, g, ny)
+        total = landed(hl, hsend, hrecv, step, g, ny)
         return [total[i * part : (i + 1) * part] for i in range(spans[g][1] // part)]
 
     def every_copy(step, j):
         to_x, to_y = peer(j)
         me = gx * ny + gy
         return pltpu.make_async_remote_copy(
-            al.at[step, me], al.at[step, me], fsend.at[step, j], frecv.at[step, j],
+            al.at[step, me], al.at[step, me], fsend.at[step], frecv.at[step],
             device_id={"gx": to_x, "gy": to_y}, device_id_type=MESH,
         )
 
     def every_start(step, matrix):
         al[step, gx * ny + gy] = pack(matrix)
-
-        def body(i, carry):
-            every_copy(step, devices - 1 - i).start()
-            return carry
-
-        lax.fori_loop(0, devices - 1, body, 0)
+        for j in reversed(range(1, devices)):
+            every_copy(step, j).start()
 
     def every_finish(step):
-        def body(j, carry):
-            every_copy(step, j).wait()
-            return carry
-
-        lax.fori_loop(1, devices, body, 0)
+        for semaphore in (fsend, frecv):
+            settle(al.at[step, pl.ds(0, devices - 1)], semaphore.at[step])
         terms = [al[step, j] for j in range(devices)]
         while len(terms) > 1:
             terms = [a + b for a, b in zip(terms[::2], terms[1::2])]
@@ -314,7 +321,7 @@
         return [
             pltpu.make_async_remote_copy(
                 from_ref, to_ref, csend.at[i], crecv.at[i],
-                device_id={axis: lax.rem(me + 1, n)}, device_id_type=MESH,
+                device_id={axis: me + 1}, device_id_type=MESH,
             )
             for i, (from_ref, to_ref, axis, me, n) in enumerate(
                 ((cond_x, xc, "gx", gx, nx), (cond_y, yc, "gy", gy, ny))
@@ -412,7 +419,7 @@
         to_x, to_y = peer(j)
         at = pl.multiple_of((to_x * ny + to_y) * SUBLANES, SUBLANES)
         return pltpu.make_async_remote_copy(
-            send.at[pl.ds(at, SUBLANES)], land.at[j], asend.at[j], arecv.at[j],
+            send.at[pl.ds(at, SUBLANES)], land.at[j], asend.at[0], arecv.at[j // together],
             device_id={"gx": to_x, "gy": to_y}, device_id_type=MESH,
         )
 
@@ -435,8 +442,6 @@
         h, col = divmod(c * LANES, low_count)
         return inj[step, h * size : (h + 1) * size, col : col + LANES]
 
-    together = 4
-
     def inject_part(step, part, parts):
         each = devices // parts
 
@@ -454,7 +459,7 @@
         ))
     ]
     fetches = [
-        pltpu.make_async_copy(v_hbm.at[:, c], v.at[c // tile_x, c % tile_x], vsem.at[c])
+        pltpu.make_async_copy(v_hbm.at[:, c], v.at[c // tile_x, c % tile_x], vsem.at[0])
         for c in range(count)
     ]
     for copy in inputs[:4] + fetches + inputs[4:]:
@@ -464,7 +469,7 @@
             for side, last in ((0, 0), (1, n - 1)):
                 @pl.when(me == last)
                 def _():
-                    to[e, side] = jnp.zeros(to.shape[2:], F32)
+                    to[e, side] = jnp.zeros(to.shape[2:], to.dtype)
 
     @pl.when(gx == 0)
     def _():
@@ -476,23 +481,20 @@
 
     barrier = pltpu.get_barrier_semaphore()
 
-    def greet(j, carry):
+    for j in range(1, devices):
+        to_x, to_y = peer(j)
         pl.semaphore_signal(
-            barrier, inc=1,
-            device_id={"gx": lax.rem(gx + j // ny, nx), "gy": lax.rem(gy + j % ny, ny)},
-            device_id_type=MESH,
+            barrier, inc=1, device_id={"gx": to_x, "gy": to_y}, device_id_type=MESH
         )
-        return carry
-
-    lax.fori_loop(1, devices, greet, 0)
     inputs[0].wait()
     find_spots()
     for copy in inputs[1:4]:
         copy.wait()
     fill_bins()
-    for copy in fetches + inputs[4:]:
+    settle(v, vsem.at[0])
+    for copy in inputs[4:]:
         copy.wait()
-    rim = Rim()
+    rim = Rim(0)
     for c in range(count):
         rim.add(c, v[c // tile_x, c % tile_x])
     pl.semaphore_wait(barrier, devices - 1)
@@ -501,13 +503,10 @@
     pl.when(gx < nx - 1)(rims[0].start)
     pl.when(gy < ny - 1)(rims[1].start)
 
-    def start_bin(i, carry):
-        bin_copy(devices - 1 - i).start()
-        return carry
-
-    lax.fori_loop(0, devices - 1, start_bin, 0)
-    start(x_copies(v, 0), gx, nx)
-    rim.send(0)
+    for j in reversed(range(1, devices)):
+        bin_copy(j).start()
+    rim.send_x()
+    rim.send_y()
     own = pl.multiple_of((gx * ny + gy) * SUBLANES, SUBLANES)
     land[0] = send[pl.ds(own, SUBLANES), :]
     wave_high, wave_low = halves(waves[...])
@@ -518,12 +517,14 @@
     inj[...] = jnp.zeros_like(inj)
 
     def first_inject(q, carry):
-        for i in range(together):
-            j = q * together + i
-            if i:
-                bin_copy(j).wait()
-            else:
-                pl.when(j > 0)(bin_copy(j).wait)
+        @pl.when(q == 0)
+        def _():
+            settle(land.at[pl.ds(1, together - 1)], arecv.at[0])
+
+        @pl.when(q > 0)
+        def _():
+            settle(land.at[pl.ds(q * together, together)], arecv.at[q])
+
         inject(0, [q * together + i for i in range(together)])
         return carry
 
@@ -534,8 +535,8 @@
     inside(v, 1, k0)
     early = nx // together
     lax.fori_loop(0, early, first_inject, 0)
-    arrive(v, 0)
-    rim = Rim()
+    arrive(0)
+    rim = Rim(1)
 
     def first_residual(c, total):
         f = -SCALE * total
@@ -546,13 +547,14 @@
 
     outside(k0, 0, first_residual, lambda: None)
     lax.fori_loop(early, devices // together, first_inject, 0)
+    settle(send.at[pl.ds(0, (devices - 1) * SUBLANES)], asend.at[0])
     for c in range(tile_x):
         f = k0[0, c] - injected(0, c)
         k0[0, c] = f
         split(0, c, f)
         rim.add(c, f)
-    start(x_copies(k0, 1), gx, nx)
-    rim.send(1)
+    rim.send_x()
+    rim.send_y()
 
     def time_step(step, carry):
         e = 1 + ITERS * step
@@ -567,10 +569,10 @@
         inside(k0, 0, k1)
         inject_next(0)
         for j in range(1, ITERS + 1):
-            arrive(fields[j - 1], e + j - 1)
+            arrive(e + j - 1)
             if j > 1:
                 add_turn(step, j - 2)
-            rim = Rim()
+            rim = Rim(e + j)
 
             def next_field(c, total):
                 split(j, c, total)
@@ -580,11 +582,11 @@
 
             def send_edges():
                 if j < ITERS:
-                    start(x_copies(fields[j], e + j), gx, nx)
+                    rim.send_x()
 
             outside(fields[j], e + j - 1, next_field, send_edges)
             if j < ITERS:
-                rim.send(e + j)
+                rim.send_y()
                 moments = moments + grams([j - 1, j], j)
                 inside(fields[j], 0, fields[j + 1])
                 add_start(step, j - 1, moments)
@@ -619,7 +621,7 @@
         high, low = halves(both)
         turned = jnp.concatenate([high.astype(F32), low.astype(F32)], axis=1).T.astype(BF16)
         turned = jnp.concatenate([turned, turned], axis=1)
-        rim = Rim()
+        rim = Rim(jnp.minimum(e + ITERS, halos - 1))
         pairs = sorted({c - c % 2 for c in edges})
         for n, c in enumerate(pairs + [c for c in range(0, count, 2) if c not in pairs]):
             out = jnp.dot(
@@ -641,26 +643,19 @@
                 split(0, c + i, left)
                 rim.add(c + i, left)
             if n + 1 == len(pairs):
-                @pl.when(more)
-                def _():
-                    start(x_copies(k0, e + ITERS), gx, nx)
-
-        @pl.when(more)
-        def _():
-            rim.send(e + ITERS)
-
+                pl.when(more)(rim.send_x)
+
+        pl.when(more)(rim.send_y)
         return carry
 
     lax.fori_loop(0, steps, time_step, 0)
-    stores = []
     for i, (here, there) in enumerate(((v, v_out), (r, r_out))):
         for c in range(count):
-            stores.append(
-                pltpu.make_async_copy(here.at[c // tile_x, c % tile_x], there.at[:, c], osem.at[i, c])
-            )
-            stores[-1].start()
-    for copy in stores:
-        copy.wait()
+            pltpu.make_async_copy(
+                here.at[c // tile_x, c % tile_x], there.at[:, c], osem.at[i]
+            ).start()
+    for i, here in enumerate((v, r)):
+        settle(here, osem.at[i])
 
 
 def hand_over_kernel(first, second, first_out, second_out, held, fetched, stored):
@@ -733,13 +728,14 @@
             pltpu.VMEM(waveforms.shape, F32),
             *[pltpu.VMEM(many, jnp.int32)] * 3,
             pltpu.VMEM(many, F32),
-            dma((9,)), dma((count,)), dma((2, count)),
+            dma((9,)), dma((1,)), dma((2,)),
             pltpu.VMEM(field, F32),
             pltpu.VMEM(field, F32),
             pltpu.VMEM(field, F32),
             pltpu.VMEM(field, F32),
             pltpu.VMEM((2 * (ITERS + 1) * size, count * LANES), BF16),
-            pltpu.VMEM((halos, 2, layers, size, LANES), F32),
+            pltpu.VMEM((halos, 2, layers, size, LANES), BF16),
+            pltpu.VMEM((halos, 2, layers, size, LANES), BF16),
             pltpu.VMEM((halos, size, LANES), F32),
             pltpu.VMEM((halos, 2, size, LANES), F32),
             pltpu.VMEM((steps, nx, packed, LANES), F32),
@@ -754,11 +750,10 @@
             pltpu.VMEM((devices, SUBLANES, LANES), F32),
             pltpu.VMEM((steps, 2 * size, waveforms.shape[1]), BF16),
             pltpu.VMEM((steps, high_count * size, low_count), F32),
-            dma((halos, 2)), dma((halos, 2)), dma((halos, 2)), dma((halos, 2)),
-            dma((steps, ITERS, nx)), dma((steps, ITERS, nx)),
-            dma((steps, ITERS, ny)), dma((steps, ITERS, ny)),
-            dma((2,)), dma((2,)), dma((devices,)), dma((devices,)),
-            dma((steps, devices)), dma((steps, devices)),
+            *[dma((2, 2))] * 4,
+            *[dma((steps, ITERS - 1))] * 4,
+            dma((2,)), dma((2,)), dma((1,)), dma((devices // 4,)),
+            dma((steps,)), dma((steps,)),
         ],
         compiler_params=pltpu.CompilerParams(
             collective_id=0, has_side_effects=True, vmem_limit_bytes=67043328

time: 68.9 us -> 62.3 us (0.904)
  Pallas kernels: 68.1 us -> 61.4 us
    pallas_call x1, Pallas kernels: 66 us -> 59.3 us  [body(): pl.pallas_call(functools.partial(grid_kernel, nx, ny, steps, layers, tile...]
where the time goes in v4:
time: 62.3 us; the launch traced here: 62 us
  Pallas kernels  61.4 us (99%)
  between operations  0.64 us (1%)
    pallas_call x1, Pallas kernels, body(): pl.pallas_call(functools.partial(grid_kernel, nx, ny, steps, layers, tile...  59.3 us
    pallas_call x1, Pallas kernels, hand_over(): pl.pallas_call(hand_over_kernel, out_shape=[jax.ShapeDtypeStruct(first.sh...  2.09 us

profile of v4, /device:TPU:0, one launch (start us, length us, event | category | flops | bytes accessed | tf_op | source)
XLA Modules:
  0.0 62.0 jit_solution(9090469659322429720)
XLA Ops:
  0.6 59.3 %transient.1 = (f32[32,32,128]{2,1,0:T(8,128)}, f32[32,32,128]{2,1,0:T(8,128)}) custom-call(f32[32,32,128]{2,1,0:T(8,128)} %bitcast.11, f32[32,128]{1,0:T(8,128)} %bitcast.16, f32[32,128]{1,0:T(8,128)} %bitcast.17, f32[32,128]{1,0:T(8,128)} %bitcast.18, f32[32,128]{1,0:T(8,128)} %bitcast.19, f32[64,64]{1,0:T(8,128)} %waves_hbm.1, s32[64,128]{1,0:T(8,128)} %bitcast.12, ...), custom_call_target="tpu_custom_call" | custom-call | tf_op jit(solution)/shard_map/transient/pallas_call | solution.py:719
  60.0 2.1 %hand_over.1 = (f32[32,32,128]{2,1,0:T(8,128)}, f32[32,32,128]{2,1,0:T(8,128)}) custom-call(f32[32,32,128]{2,1,0:T(8,128)} %get-tuple-element.6.first, f32[32,32,128]{2,1,0:T(8,128)} %get-tuple-element.7.second), custom_call_target="tpu_custom_call" | custom-call | tf_op jit(solution)/shard_map/hand_over/pallas_call | solution.py:689

commit v5 on v4

--- a/solution.py
+++ b/solution.py
@@ -101,7 +101,7 @@
     v_out, r_out,
     v, r, cap, cond_x, cond_y, via, waves, target, cells, kinds, amps, isem, vsem, osem,
     k0, k1, k2, k3, basis, xs, xl, ys, yl, gl, hl, al,
-    coef, xc, yc, spots, bins, send, land, table, inj,
+    coef, strip, xc, yc, spots, bins, send, land, table, inj,
     xsend, xrecv, ysend, yrecv, gsend, grecv, hsend, hrecv, csend, crecv, asend, arecv, fsend, frecv,
 ):
     gx, gy = lax.axis_index("gx"), lax.axis_index("gy")
@@ -246,6 +246,27 @@
             product[2 * i * size : (2 * i + 1) * size] + product[(2 * i + 1) * size : (2 * i + 2) * size]
             for i in range(len(left))
         ]
+
+    def rim_gram(e):
+        beyond = jnp.where(
+            lane % 2 == 0, pltpu.roll(yl[e, 1], LANES - 1, 1), pltpu.roll(yl[e, 0], 1, 1)
+        )
+        left, right = [halves(ys[e])], [halves(-(strip[:1] * beyond))]
+        for c in edges:
+            l, x = divmod(c, tile_x)
+            side, i = (1, 2) if x else (0, 3)
+            cols = slice(c * LANES, (c + 1) * LANES)
+            left.append([
+                basis[b * size : (b + 1) * size, cols] for b in (ITERS - 1, 2 * ITERS)
+            ])
+            right.append(halves(-(k(i, c) * xl[e, side, l].astype(F32))))
+        left, right = (
+            jnp.concatenate([jnp.concatenate(part, axis=0) for part in parts], axis=1)
+            for parts in (left, right)
+        )
+        product = lax.dot_general(left, right, NT, preferred_element_type=F32)
+        product = product[:, :size] + product[:, size:]
+        return product[:size] + product[size:]
 
     def pack(matrix):
         return jnp.concatenate([matrix[i * part : (i + 1) * part] for i in range(packed)], axis=1)
@@ -351,6 +372,10 @@
             for i, value in enumerate(values):
                 coef[i, at] = value
             above = via[at]
+        ends = jnp.zeros((1, LANES), F32)
+        for c in range(count):
+            ends = jnp.where(lane[:1] // 2 == c, pltpu.roll(k(8, c), 2 * c + 1, 1), ends)
+        strip[:1] = ends
 
     def find_spots():
         width = 2 * LANES
@@ -570,7 +595,8 @@
         inject_next(0)
         for j in range(1, ITERS + 1):
             arrive(e + j - 1)
-            if j > 1:
+            if j == ITERS:
+                every_start(step, near + rim_gram(e + j - 1))
                 add_turn(step, j - 2)
             rim = Rim(e + j)
 
@@ -588,11 +614,15 @@
             if j < ITERS:
                 rim.send_y()
                 moments = moments + grams([j - 1, j], j)
+                add_start(step, j - 1, moments)
+                if j > 1:
+                    add_turn(step, j - 2)
                 inside(fields[j], 0, fields[j + 1])
-                add_start(step, j - 1, moments)
                 moments = []
-            else:
-                every_start(step, grams([j - 1], j)[0])
+            if j == ITERS - 1:
+                for c in range(count):
+                    split(ITERS, c, k3[c // tile_x, c % tile_x])
+                (near,) = grams([j], ITERS)
             inject_next(j)
         m = add_finish(step, 0) + add_finish(step, 1)
         m.append(jnp.zeros_like(m[0]))
@@ -742,6 +772,7 @@
             pltpu.VMEM((steps, ny, packed, LANES), F32),
             pltpu.VMEM((steps, devices, size * size // LANES, LANES), F32),
             pltpu.VMEM((10,) + flat, F32),
+            pltpu.VMEM((SUBLANES, LANES), F32),
             pltpu.VMEM(flat, F32),
             pltpu.VMEM(flat, F32),
             pltpu.VMEM(many, jnp.int32),

time: 62.3 us -> 60.8 us (0.976)
  Pallas kernels: 61.4 us -> 60 us
    pallas_call x1, Pallas kernels: 59.3 us -> 57.9 us  [body(): pl.pallas_call(functools.partial(grid_kernel, nx, ny, steps, layers, tile...]
where the time goes in v5:
time: 60.8 us; the launch traced here: 60.6 us
  Pallas kernels  60 us (99%)
  between operations  0.64 us (1%)
    pallas_call x1, Pallas kernels, body(): pl.pallas_call(functools.partial(grid_kernel, nx, ny, steps, layers, tile...  57.9 us
    pallas_call x1, Pallas kernels, hand_over(): pl.pallas_call(hand_over_kernel, out_shape=[jax.ShapeDtypeStruct(first.sh...  2.09 us

profile of v5, /device:TPU:0, one launch (start us, length us, event | category | flops | bytes accessed | tf_op | source)
XLA Modules:
  0.0 60.6 jit_solution(13654027432332715105)
XLA Ops:
  0.6 57.9 %transient.1 = (f32[32,32,128]{2,1,0:T(8,128)}, f32[32,32,128]{2,1,0:T(8,128)}) custom-call(f32[32,32,128]{2,1,0:T(8,128)} %bitcast.11, f32[32,128]{1,0:T(8,128)} %bitcast.16, f32[32,128]{1,0:T(8,128)} %bitcast.17, f32[32,128]{1,0:T(8,128)} %bitcast.18, f32[32,128]{1,0:T(8,128)} %bitcast.19, f32[64,64]{1,0:T(8,128)} %waves_hbm.1, s32[64,128]{1,0:T(8,128)} %bitcast.12, ...), custom_call_target="tpu_custom_call" | custom-call | tf_op jit(solution)/shard_map/transient/pallas_call | solution.py:749
  58.5 2.1 %hand_over.1 = (f32[32,32,128]{2,1,0:T(8,128)}, f32[32,32,128]{2,1,0:T(8,128)}) custom-call(f32[32,32,128]{2,1,0:T(8,128)} %get-tuple-element.6.first, f32[32,32,128]{2,1,0:T(8,128)} %get-tuple-element.7.second), custom_call_target="tpu_custom_call" | custom-call | tf_op jit(solution)/shard_map/hand_over/pallas_call | solution.py:719

commit v6 on v5

--- a/solution.py
+++ b/solution.py
@@ -487,23 +487,7 @@
         pltpu.make_async_copy(v_hbm.at[:, c], v.at[c // tile_x, c % tile_x], vsem.at[0])
         for c in range(count)
     ]
-    for copy in inputs[:4] + fetches + inputs[4:]:
-        copy.start()
-    for e in range(halos):
-        for me, n, to in ((gx, nx, xl), (gy, ny, yl)):
-            for side, last in ((0, 0), (1, n - 1)):
-                @pl.when(me == last)
-                def _():
-                    to[e, side] = jnp.zeros(to.shape[2:], to.dtype)
-
-    @pl.when(gx == 0)
-    def _():
-        xc[...] = jnp.zeros_like(xc)
-
-    @pl.when(gy == 0)
-    def _():
-        yc[...] = jnp.zeros_like(yc)
-
+    inputs[0].start()
     barrier = pltpu.get_barrier_semaphore()
 
     for j in range(1, devices):
@@ -511,6 +495,23 @@
         pl.semaphore_signal(
             barrier, inc=1, device_id={"gx": to_x, "gy": to_y}, device_id_type=MESH
         )
+    for copy in inputs[1:4] + fetches + inputs[4:]:
+        copy.start()
+    for me, n, to in ((gx, nx, xl), (gy, ny, yl)):
+        for side, last in ((0, 0), (1, n - 1)):
+            @pl.when(me == last)
+            def _():
+                for e in range(halos):
+                    to[e, side] = jnp.zeros(to.shape[2:], to.dtype)
+
+    @pl.when(gx == 0)
+    def _():
+        xc[...] = jnp.zeros_like(xc)
+
+    @pl.when(gy == 0)
+    def _():
+        yc[...] = jnp.zeros_like(yc)
+
     inputs[0].wait()
     find_spots()
     for copy in inputs[1:4]:

time: 60.8 us -> 60.6 us (level)
  no operation moved by 1% of the time
where the time goes in v6:
time: 60.6 us; the launch traced here: 60.4 us
  Pallas kernels  59.8 us (99%)
  between operations  0.64 us (1%)
    pallas_call x1, Pallas kernels, body(): pl.pallas_call(functools.partial(grid_kernel, nx, ny, steps, layers, tile...  57.7 us
    pallas_call x1, Pallas kernels, hand_over(): pl.pallas_call(hand_over_kernel, out_shape=[jax.ShapeDtypeStruct(first.sh...  2.09 us

profile of v6, /device:TPU:0, one launch (start us, length us, event | category | flops | bytes accessed | tf_op | source)
XLA Modules:
  0.0 60.4 jit_solution(3959876959671757959)
XLA Ops:
  0.6 57.7 %transient.1 = (f32[32,32,128]{2,1,0:T(8,128)}, f32[32,32,128]{2,1,0:T(8,128)}) custom-call(f32[32,32,128]{2,1,0:T(8,128)} %bitcast.11, f32[32,128]{1,0:T(8,128)} %bitcast.16, f32[32,128]{1,0:T(8,128)} %bitcast.17, f32[32,128]{1,0:T(8,128)} %bitcast.18, f32[32,128]{1,0:T(8,128)} %bitcast.19, f32[64,64]{1,0:T(8,128)} %waves_hbm.1, s32[64,128]{1,0:T(8,128)} %bitcast.12, ...), custom_call_target="tpu_custom_call" | custom-call | tf_op jit(solution)/shard_map/transient/pallas_call | solution.py:750
  58.3 2.1 %hand_over.1 = (f32[32,32,128]{2,1,0:T(8,128)}, f32[32,32,128]{2,1,0:T(8,128)}) custom-call(f32[32,32,128]{2,1,0:T(8,128)} %get-tuple-element.6.first, f32[32,32,128]{2,1,0:T(8,128)} %get-tuple-element.7.second), custom_call_target="tpu_custom_call" | custom-call | tf_op jit(solution)/shard_map/hand_over/pallas_call | solution.py:720
